TPU v7x, 256 devices: a whole 4x4x8 slice. The times are simulated.
256 devices in a mesh: dp: 32 (over y, z_hi, x), tensor: 8 (over z_lo, core).
Axes of the slice: x: 4, y: 4, z: 8 (z_hi: 2, z_lo: 4; z = z_hi * 4 + z_lo), core: 2. Of those that a mesh axis runs over, the one named last changes fastest.
Arguments:
- tokens: bfloat16 [1536, 6144], P('dp', 'tensor'), may hold values from -6 to 6
- out_grad: bfloat16 [1536, 6144], P('dp', 'tensor'), may hold values from -1.5 to 1.5
- expert_ids: int32 [1536, 2], P('dp'), may hold values from 0 to 3, all different within a row; in each aligned block of 48 rows (0 to 47, 48 to 95, ...) at most 32 rows name the same one
- gate_prob: bfloat16 [1536, 2], P('dp'), may hold values from 0.19921875 to 1
- gate_weight: bfloat16 [6144, 32768], P('tensor', 'dp'), may hold values from -0.078125 to 0.078125
- up_weight: bfloat16 [6144, 32768], P('tensor', 'dp'), may hold values from -0.078125 to 0.078125
- down_weight: bfloat16 [32768, 6144], P('dp', 'tensor'), may hold values from -0.0625 to 0.0625
Outputs:
- input_grad: bfloat16 [1536, 6144], P('dp', 'tensor')
- prob_grad: float32 [1536, 2], P('dp')
- gate_grad: bfloat16 [6144, 32768], P('tensor', 'dp')
- up_grad: bfloat16 [6144, 32768], P('tensor', 'dp')
- down_grad: bfloat16 [32768, 6144], P('dp', 'tensor')
Inputs may be any that keep to these rules, and one draw needn't show every extreme that they name: `expert_ids`: the two ids of a token differ. Among the 48 tokens of one index of dp (aligned blocks of rows), no expert is named by more than 32 tokens, a bound that some block reaches.
All inputs are finite; a program needn't handle non-finite values.
Results may differ from a plain program's by a relative error of at most 0.0057.
Values may be sent and summed in bfloat16 or wider, within the bound.
A program may use at most 128 MiB of HBM per device.

v0:
```python
import jax
import jax.numpy as jnp
from jax import lax
from jax.sharding import PartitionSpec as P

EXPERTS = 4
CAP = 32


precise = lax.Precision.HIGHEST


def sent_together(arrays, axis, dim, along):
    widths = [a.shape[along] for a in arrays]
    both = jnp.concatenate(arrays, axis=along)
    result = lax.psum_scatter(both, axis, scatter_dimension=dim, tiled=True)
    return tuple(jnp.split(result, [sum(widths[:k]) for k in range(1, len(widths))], axis=along))


def side_by_side(arrays, axis, dim, along):
    ends, at = ([], 0)
    for a in arrays[:-1]:
        at += a.shape[along]
        ends.append(at)
    both = jnp.concatenate(arrays, axis=along)
    return tuple(jnp.split(lax.all_gather(both, axis, axis=dim, tiled=True), ends, axis=along))


def slot_table(expert_ids):
    labels = expert_ids.reshape(-1)
    onehot = (labels[:, None] == jnp.arange(EXPERTS, dtype=jnp.int32)[None, :]).astype(jnp.int32)
    before = jnp.cumsum(onehot, axis=0) - onehot
    places = jnp.sum(before * onehot, axis=1)
    codes = labels * CAP + places
    return jnp.arange(EXPERTS * CAP, dtype=jnp.int32)[:, None] == codes[None, :]


def inner_rows(left, right):
    return lax.dot_general(
        left, right, (((0,), (0,)), ((), ())), preferred_element_type=jnp.float32
    )


def times_transposed(left, right):
    return lax.dot_general(
        left, right, (((1,), (1,)), ((), ())), preferred_element_type=jnp.float32
    )


def body(tokens, out_grad, expert_ids, gate_prob, gate_weight, up_weight, down_weight):
    dp_count = lax.axis_size("dp")
    group_size = dp_count // EXPERTS
    part_width = tokens.shape[1]
    selector = slot_table(expert_ids)
    token_pick = jnp.any(selector.reshape(EXPERTS * CAP, -1, 2), axis=2).astype(jnp.bfloat16)
    slot_pick = selector.astype(jnp.bfloat16)
    send_rows = (
        jnp.dot(token_pick, tokens, preferred_element_type=jnp.float32)
        .astype(jnp.bfloat16)
        .reshape(EXPERTS, CAP, part_width)
    )
    send_grads = (
        jnp.dot(token_pick, out_grad, preferred_element_type=jnp.float32)
        .astype(jnp.bfloat16)
        .reshape(EXPERTS, CAP, part_width)
    )
    send_probs = (
        jnp.dot(slot_pick, gate_prob.reshape(-1, 1), preferred_element_type=jnp.float32)
        .astype(jnp.bfloat16)
        .reshape(EXPERTS, CAP)
    )
    arrived_rows, arrived_grads, arrived_probs = (
        lax.all_to_all(
            jnp.repeat(send_rows, group_size, axis=0), "dp", split_axis=0, concat_axis=0, tiled=True
        ),
        lax.all_to_all(
            jnp.repeat(send_grads, group_size, axis=0),
            "dp",
            split_axis=0,
            concat_axis=0,
            tiled=True,
        ),
        lax.all_to_all(
            jnp.repeat(send_probs, group_size, axis=0),
            "dp",
            split_axis=0,
            concat_axis=0,
            tiled=True,
        ),
    )
    routed_rows = arrived_rows.reshape(-1, part_width)
    routed_grads = arrived_grads.reshape(-1, part_width)
    routed_probs = arrived_probs.reshape(-1).astype(jnp.float32)
    part_gate = jnp.dot(routed_rows, gate_weight, preferred_element_type=jnp.float32)
    part_up = jnp.dot(routed_rows, up_weight, preferred_element_type=jnp.float32)
    part_back = times_transposed(routed_grads, down_weight)
    pre_gate, pre_up, back_hidden = sent_together((part_gate, part_up, part_back), "tensor", 1, 0)
    sigmoid_gate = jax.nn.sigmoid(pre_gate)
    hidden_share = (pre_gate * sigmoid_gate * pre_up).astype(jnp.bfloat16)
    hidden_grad = routed_probs[:, None] * back_hidden
    gate_share = (
        hidden_grad * pre_up * sigmoid_gate * (1.0 + pre_gate * (1.0 - sigmoid_gate))
    ).astype(jnp.bfloat16)
    up_share = (hidden_grad * pre_gate * sigmoid_gate).astype(jnp.bfloat16)
    hidden, gate_pre, up_pre = side_by_side((hidden_share, gate_share, up_share), "tensor", 1, 0)
    prob_term = lax.psum(jnp.sum(hidden_share.astype(jnp.float32) * back_hidden, axis=1), "tensor")
    input_part = times_transposed(gate_pre, gate_weight) + times_transposed(up_pre, up_weight)
    scaled = (routed_probs[:, None] * routed_grads.astype(jnp.float32)).astype(jnp.bfloat16)
    gate_grad = inner_rows(routed_rows, gate_pre).astype(jnp.bfloat16)
    up_grad = inner_rows(routed_rows, up_pre).astype(jnp.bfloat16)
    down_grad = inner_rows(hidden, scaled).astype(jnp.bfloat16)
    back_rows, back_probs = (
        lax.all_to_all(
            input_part.reshape(dp_count, CAP, part_width),
            "dp",
            split_axis=0,
            concat_axis=0,
            tiled=True,
        ),
        lax.all_to_all(
            prob_term.reshape(dp_count, CAP), "dp", split_axis=0, concat_axis=0, tiled=True
        ),
    )
    summed_rows = jnp.sum(back_rows.reshape(EXPERTS, group_size, CAP, part_width), axis=1).reshape(
        EXPERTS * CAP, part_width
    )
    summed_probs = jnp.sum(back_probs.reshape(EXPERTS, group_size, CAP), axis=1).reshape(
        EXPERTS * CAP
    )
    input_grad = lax.dot_general(
        token_pick.astype(jnp.float32),
        summed_rows,
        (((0,), (0,)), ((), ())),
        precision=precise,
        preferred_element_type=jnp.float32,
    ).astype(jnp.bfloat16)
    prob_grad = lax.dot_general(
        slot_pick.astype(jnp.float32),
        summed_probs,
        (((0,), (0,)), ((), ())),
        precision=precise,
        preferred_element_type=jnp.float32,
    ).reshape(-1, 2)
    return (input_grad, prob_grad, gate_grad, up_grad, down_grad)


def solution(mesh):
    return jax.shard_map(
        body,
        mesh=mesh,
        in_specs=(
            P("dp", "tensor"),
            P("dp", "tensor"),
            P("dp", None),
            P("dp", None),
            P("tensor", "dp"),
            P("tensor", "dp"),
            P("dp", "tensor"),
        ),
        out_specs=(
            P("dp", "tensor"),
            P("dp", None),
            P("tensor", "dp"),
            P("tensor", "dp"),
            P("dp", "tensor"),
        ),
        check_vma=False,
    )
```

profile of v0, /device:TPU:1, one launch (start us, length us, event | category | flops | bytes accessed | tf_op | source)
XLA Modules:
  0.0 427.6 jit_solution(15862091266998034014)
XLA Ops:
  7.2 0.9 copy.41
  8.8 0.7 multiply_add_fusion
  9.6 1.1 convolution_convert_fusion.1
  10.7 1.3 broadcast_in_dim.6
  12.1 14.6 %all-to-all-start = ((bf16[32,32,768]{2,1,0:T(8,128)(2,1)}), bf16[32,32,768]{2,1,0:T(8,128)(2,1)S(1)}, u32[]{:S(2)}, u32[]{:S(2)}) async-start(bf16[32,32,768]{2,1,0:T(8,128)(2,1)} %bitcast.1), calls=%async_computation | async-start | bytes 3145728 | tf_op jit(solution)/shard_map/all_to_all | solution.py:73
  27.0 28.5 %all-to-all-done = bf16[32,32,768]{2,1,0:T(8,128)(2,1)S(1)} async-done(((bf16[32,32,768]{2,1,0:T(8,128)(2,1)}), bf16[32,32,768]{2,1,0:T(8,128)(2,1)S(1)}, u32[]{:S(2)}, u32[]{:S(2)}) %all-to-all-start) | async-done | bytes 1572896 | tf_op jit(solution)/shard_map/all_to_all | solution.py:73
  55.4 1.3 broadcast_in_dim.7
  56.7 4.7 %all-to-all-start.1 = ((bf16[32,32,768]{2,1,0:T(8,128)(2,1)}), bf16[32,32,768]{2,1,0:T(8,128)(2,1)}, u32[]{:S(2)}, u32[]{:S(2)}) async-start(bf16[32,32,768]{2,1,0:T(8,128)(2,1)} %bitcast.4), calls=%async_computation.1 | async-start | bytes 3145728 | tf_op jit(solution)/shard_map/all_to_all | solution.py:76
  61.5 5.2 %fusion.29 = f32[1024,1024]{1,0:T(8,128)} fusion(bf16[1024,768]{1,0:T(8,128)(2,1)S(1)} %bitcast.41, bf16[768,1024]{1,0:T(8,128)(2,1)} %param.11), kind=kOutput, calls=%fused_computation.45 | convolution fusion | flops 1610612736 | bytes 7340032 | tf_op jit(solution)/shard_map/dot_general | solution.py:94
  66.7 3.7 fusion.30
  70.4 8.7 %all-to-all-done.1 = bf16[32,32,768]{2,1,0:T(8,128)(2,1)} async-done(((bf16[32,32,768]{2,1,0:T(8,128)(2,1)}), bf16[32,32,768]{2,1,0:T(8,128)(2,1)}, u32[]{:S(2)}, u32[]{:S(2)}) %all-to-all-start.1) | async-done | bytes 1572896 | tf_op jit(solution)/shard_map/all_to_all | solution.py:76
  79.1 3.8 fusion.31
  83.0 0.5 copy-done.2
  83.6 5.6 %pad_maximum_fusion = f32[3072,1024]{1,0:T(8,128)} fusion(f32[1024,1024]{1,0:T(8,128)S(1)} %fusion.31, f32[1024,1024]{1,0:T(8,128)S(1)} %copy-done.2, f32[1024,1024]{1,0:T(8,128)S(1)} %copy-done.1), kind=kLoop, calls=%fused_computation | loop fusion | flops 6291456 | bytes 25165824 | tf_op jit(solution)/shard_map/concatenate | solution.py:15
  89.2 0.6 copy-done.4
  90.3 20.1 %all_to_all.33 = bf16[32,1,32]{2,1,0:T(2,128)(2,1)S(1)} all-to-all(bf16[32,1,32]{2,1,0:T(2,128)(2,1)S(1)} %copy.44), channel_id=1, replica_groups=mesh['dp'=32,'tensor'=8] {'dp'}, dimensions={0} | all-to-all | bytes 4096 | tf_op jit(solution)/shard_map/all_to_all | solution.py:83
  110.5 135.9 %reduce-scatter.2.cloned.1.call-done = f32[3072,128]{1,0:T(8,128)} async-done(((f32[3072,1024]{1,0:T(8,128)}), f32[3072,128]{1,0:T(8,128)}) %reduce-scatter.2.cloned.1.call-update) | async-done | bytes 1572880 | tf_op jit(solution)/shard_map/reduce_scatter | solution.py:16
  246.4 1.8 multiply_reduce_fusion
  248.2 0.9 pad_maximum_fusion.1
  249.3 25.4 %psum.7 = f32[32,1,32]{2,1,0:T(1,128)} all-reduce(f32[32,1,32]{2,1,0:T(1,128)S(1)} %all_to_all.26), channel_id=1, replica_groups=mesh['dp'=32,'tensor'=8] {'tensor'}, use_global_device_ids=true, to_apply=%region_6.7 | all-reduce | flops 1024 | bytes 8192 | tf_op jit(solution)/shard_map/psum | solution.py:106
  274.6 11.9 %all-to-all-start.4 = ((f32[32,1,32]{2,1,0:T(1,128)}), f32[32,1,32]{2,1,0:T(1,128)S(1)}, u32[]{:S(2)}, u32[]{:S(2)}) async-start(f32[32,1,32]{2,1,0:T(1,128)} %psum.7), calls=%async_computation.5 | async-start | bytes 32768 | tf_op jit(solution)/shard_map/all_to_all | solution.py:120
  286.5 38.2 %all-gather.2.cloned.1.call-done = bf16[3072,1024]{1,0:T(8,128)(2,1)} async-done(((bf16[3072,128]{1,0:T(8,128)(2,1)}), bf16[3072,1024]{1,0:T(8,128)(2,1)}) %all-gather.2.cloned.1.call-update) | async-done | bytes 6291472 | tf_op jit(solution)/shard_map/all_gather | solution.py:26
  324.7 3.6 fusion.4
  328.5 3.5 fusion.10
  332.0 10.9 %all-to-all-start.3 = ((f32[32,32,768]{2,1,0:T(8,128)}), f32[32,32,768]{2,1,0:T(8,128)}, u32[]{:S(2)}, u32[]{:S(2)}) async-start(f32[32,32,768]{2,1,0:T(8,128)} %bitcast.40), calls=%async_computation.4 | async-start | bytes 6291456 | tf_op jit(solution)/shard_map/all_to_all | solution.py:113
  343.2 0.8 fusion.26
  344.0 4.6 %fusion.13 = bf16[768,1024]{1,0:T(8,128)(2,1)} fusion(bf16[1024,768]{1,0:T(8,128)(2,1)S(1)} %bitcast.43, bf16[3072,1024]{1,0:T(8,128)(2,1)} %all-gather.2.cloned.1.call-done), kind=kOutput, calls=%fused_computation.14 | convolution fusion | flops 1611399168 | bytes 5242880 | tf_op jit(solution)/shard_map/dot_general | solution.py:39
  348.5 4.6 %fusion.16 = bf16[768,1024]{1,0:T(8,128)(2,1)} fusion(bf16[1024,768]{1,0:T(8,128)(2,1)S(1)} %bitcast.44, bf16[3072,1024]{1,0:T(8,128)(2,1)} %all-gather.2.cloned.1.call-done), kind=kOutput, calls=%fused_computation.15 | convolution fusion | flops 1611399168 | bytes 5242880 | tf_op jit(solution)/shard_map/dot_general | solution.py:39
  353.1 5.2 %fusion.19 = bf16[1024,768]{1,0:T(8,128)(2,1)} fusion(bf16[3072,1024]{1,0:T(8,128)(2,1)} %all-gather.2.cloned.1.call-done, bf16[1024,768]{1,0:T(8,128)(2,1)} %bitcast.5, f32[1024]{0:T(1024)S(1)} %reshape.131), kind=kOutput, calls=%fused_computation.16 | convolution fusion | flops 1613758464 | bytes 5246976 | tf_op jit(solution)/shard_map/dot_general | solution.py:39
  358.3 59.4 %all-to-all-done.3 = f32[32,32,768]{2,1,0:T(8,128)} async-done(((f32[32,32,768]{2,1,0:T(8,128)}), f32[32,32,768]{2,1,0:T(8,128)}, u32[]{:S(2)}, u32[]{:S(2)}) %all-to-all-start.3) | async-done | bytes 3145760 | tf_op jit(solution)/shard_map/all_to_all | solution.py:113
  417.7 2.1 bitcast_reduce_fusion
  419.8 0.9 convolution_convert_fusion.2
  (39 shorter events, 2.4 us)
Async XLA Ops:
  7.2 59.5 %copy-start = (bf16[768,1024]{1,0:T(8,128)(2,1)S(1)}, bf16[768,1024]{1,0:T(8,128)(2,1)}, u32[]{:S(2)}) copy-start(bf16[768,1024]{1,0:T(8,128)(2,1)} %param.12) | copy-start | bytes 4718596
  12.1 14.6 %copy-start.3 = (bf16[48,768]{1,0:T(8,128)(2,1)S(1)}, bf16[48,768]{1,0:T(8,128)(2,1)}, u32[]{:S(2)}) copy-start(bf16[48,768]{1,0:T(8,128)(2,1)} %param.8) | copy-start | bytes 221188
  12.1 43.4 %all-to-all-start = ((bf16[32,32,768]{2,1,0:T(8,128)(2,1)}), bf16[32,32,768]{2,1,0:T(8,128)(2,1)S(1)}, u32[]{:S(2)}, u32[]{:S(2)}) async-start(bf16[32,32,768]{2,1,0:T(8,128)(2,1)} %bitcast.1), calls=%async_computation | async-start | bytes 3145728 | tf_op jit(solution)/shard_map/all_to_all | solution.py:73
  56.7 22.4 %all-to-all-start.1 = ((bf16[32,32,768]{2,1,0:T(8,128)(2,1)}), bf16[32,32,768]{2,1,0:T(8,128)(2,1)}, u32[]{:S(2)}, u32[]{:S(2)}) async-start(bf16[32,32,768]{2,1,0:T(8,128)(2,1)} %bitcast.4), calls=%async_computation.1 | async-start | bytes 3145728 | tf_op jit(solution)/shard_map/all_to_all | solution.py:76
  61.5 184.9 %reduce-scatter.2.cloned.1.call-start = ((), (), s32[]{:S(2)}) async-start(), calls=%async_computation.6 | async-start | bytes 14155776 | tf_op jit(solution)/shard_map/reduce_scatter | solution.py:16
  79.1 3.9 copy-start.1
  79.1 4.4 %copy-start.2 = (f32[1024,1024]{1,0:T(8,128)S(1)}, f32[1024,1024]{1,0:T(8,128)}, u32[]{:S(2)}) copy-start(f32[1024,1024]{1,0:T(8,128)} %fusion.30) | copy-start | bytes 12582916
  89.1 0.7 copy-start.4
  89.1 235.5 %all-gather.2.cloned.1.call-start = ((), (), s32[]{:S(2)}) async-start(), calls=%async_computation.7 | async-start | bytes 7077888 | tf_op jit(solution)/shard_map/all_gather | solution.py:26
  274.6 57.4 %all-to-all-start.4 = ((f32[32,1,32]{2,1,0:T(1,128)}), f32[32,1,32]{2,1,0:T(1,128)S(1)}, u32[]{:S(2)}, u32[]{:S(2)}) async-start(f32[32,1,32]{2,1,0:T(1,128)} %psum.7), calls=%async_computation.5 | async-start | bytes 32768 | tf_op jit(solution)/shard_map/all_to_all | solution.py:120
  324.7 3.6 copy-start.5
  324.7 3.9 copy-start.6
  332.0 85.7 %all-to-all-start.3 = ((f32[32,32,768]{2,1,0:T(8,128)}), f32[32,32,768]{2,1,0:T(8,128)}, u32[]{:S(2)}, u32[]{:S(2)}) async-start(f32[32,32,768]{2,1,0:T(8,128)} %bitcast.40), calls=%async_computation.4 | async-start | bytes 6291456 | tf_op jit(solution)/shard_map/all_to_all | solution.py:113
Sparse Core Ops, SparseCore 0:
  89.3 157.0 reduce-scatter.1
  249.3 75.3 all-gather.1
where the time goes:
time: 431 us; the launch traced here: 428 us
  waiting for transfers between devices  271 us (63%)
  blocking collectives  45.4 us (11%)
  starting transfers between devices  42.2 us (10%)
  matrix products  37.4 us (9%)
  between operations  14.2 us (3%)
  other arithmetic  11.7 us (3%)
  local copies, waits for them, and re-layouts  5.9 us (1%)
    reduce_scatter x1, waiting for transfers between devices, sent_together(): result = lax.psum_scatter(both, axis, scatter_dimension=dim, tiled=True)  136 us
    all_to_all x1, waiting for transfers between devices, body(): lax.all_to_all(input_part.reshape(dp_count, CAP, part_width), 'dp', split...  59.4 us
    all_gather x1, waiting for transfers between devices, side_by_side(): lax.all_gather(both, axis, axis=dim, tiled=True)  38.2 us
    all_to_all x1, waiting for transfers between devices, body(): lax.all_to_all(jnp.repeat(send_rows, group_size, axis=0), 'dp', split_axi...  28.5 us
    psum x1, blocking collectives, body(): lax.psum(jnp.sum(hidden_share.astype(jnp.float32) * back_hidden, axis=1),...  25.4 us
    all_to_all x1, blocking collectives, body(): lax.all_to_all(jnp.repeat(send_probs, group_size, axis=0), 'dp', split_ax...  20.1 us
    all_to_all x1, starting transfers between devices, body(): lax.all_to_all(jnp.repeat(send_rows, group_size, axis=0), 'dp', split_axi...  14.6 us
    dot_general x3, matrix products, inner_rows(): lax.dot_general(left, right, (((0,), (0,)), ((), ())), preferred_element_...  14.4 us
  transfers between devices with their start and end apart: 6, of which 5 were waited for; matrix products, arithmetic and copies ran while one was open for 8% of the time, Pallas kernels for 0%

commit v1 on v0

v1 whole, which is shorter than its diff:
```python
import functools

import jax
import jax.numpy as jnp
from jax import lax
from jax.experimental import pallas as pl
from jax.experimental.pallas import tpu as pltpu
from jax.sharding import PartitionSpec as P

EXPERTS = 4
CAP = 32
CHUNKS = 8
ROWS = EXPERTS * CAP
SUB = 32
PER = ROWS // SUB
NSUB = CHUNKS * PER
LAG = 2
QUARTER = 256
MESH = pl.DeviceIdType.MESH
F32 = jnp.float32
BF16 = jnp.bfloat16


def dot(a, b):
    return lax.dot_general(a, b, (((1,), (0,)), ((), ())), preferred_element_type=F32)


def dot_nt(a, b):
    return lax.dot_general(a, b, (((1,), (1,)), ((), ())), preferred_element_type=F32)


def dot_tn(a, b):
    return lax.dot_general(a, b, (((0,), (0,)), ((), ())), preferred_element_type=F32)


def kernel(
    width,
    x_ref,
    p_ref,
    wg_ref,
    wu_ref,
    wd_ref,
    out_x,
    out_p,
    out_g,
    out_u,
    out_d,
    x_other,
    p_other,
    rows,
    y_send,
    w_in,
    w_out,
    own,
    pair_send,
    pair_recv,
    line,
    hid,
    ret_send,
    ret_recv,
    pick,
    z_send,
    z_recv,
    acc_in,
    acc_out,
    turned,
    w_sem,
    z_s,
    z_r,
    y_s,
    y_r,
    x_s,
    x_r,
    pair_s,
    pair_r,
    line_s,
    line_r,
    cast_s,
    cast_r,
    core_s,
    core_r,
    ret_s,
    ret_r,
    last_s,
    last_r,
):
    dp = lax.axis_index("dp")
    tensor = lax.axis_index("tensor")
    y, zh, x = dp // 8, (dp // 4) % 2, dp % 4
    zl, core = tensor // 2, tensor % 2
    here = y * 4 + x
    lanes = 2 * width

    def at(y_, zh_, x_):
        return ((y_ * 2 + zh_) * 4 + x_, tensor)

    def plane(j):
        return at(j // 4, zh, j % 4)

    other_z = at(y, 1 - zh, x)
    partner = (dp, zl * 2 + 1 - core)
    above = (dp, (tensor + 2) % 8)
    below = (dp, (tensor + 6) % 8)

    def remote(src, dst, send, recv, device):
        return pltpu.make_async_remote_copy(
            src_ref=src, dst_ref=dst, send_sem=send, recv_sem=recv, device_id=device, device_id_type=MESH
        )

    w_copies = []
    for q in range(4):
        cols = pl.ds(q * QUARTER, QUARTER)
        w_copies.append(
            pltpu.make_async_copy(wg_ref.at[:, cols], w_in.at[q, :, pl.ds(0, QUARTER)], w_sem.at[2 * q])
        )
        w_copies.append(
            pltpu.make_async_copy(
                wu_ref.at[:, cols], w_in.at[q, :, pl.ds(QUARTER, QUARTER)], w_sem.at[2 * q + 1]
            )
        )
    w_copies.append(pltpu.make_async_copy(wd_ref, w_out, w_sem.at[8]))
    for copy in w_copies:
        copy.start()

    barrier = pltpu.get_barrier_semaphore()
    for o in range(1, 16):
        pl.semaphore_signal(barrier, inc=1, device_id=plane((here + o) % 16), device_id_type=MESH)
    pl.semaphore_signal(barrier, inc=1, device_id=other_z, device_id_type=MESH)
    pl.semaphore_signal(barrier, inc=1, device_id=partner, device_id_type=MESH)

    pl.semaphore_signal(barrier, inc=1, device_id=above, device_id_type=MESH)
    pl.semaphore_signal(barrier, inc=1, device_id=below, device_id_type=MESH)
    pl.semaphore_wait(barrier, 19)

    raw = [
        remote(x_ref, x_other, z_s.at[0], z_r.at[0], other_z),
        remote(p_ref, p_other, z_s.at[1], z_r.at[1], other_z),
    ]
    for copy in raw:
        copy.start()

    def y_copy(z, o):
        to = (y + o) % 4
        return remote(
            y_send.at[z, pl.ds(to * CAP, CAP)],
            rows.at[3 * z, pl.ds(y * CAP, CAP)],
            y_s.at[z, to],
            y_r.at[z, y],
            at(to, zh, x),
        )

    def y_wait(z, o):
        source = (y + o) % 4
        remote(
            y_send.at[z, pl.ds(source * CAP, CAP)],
            rows.at[3 * z, pl.ds(source * CAP, CAP)],
            y_s.at[z, source],
            y_r.at[z, source],
            at(source, zh, x),
        ).wait_recv()

    def choose(z, xs, ps):
        p = ps[...].astype(F32)
        one = jnp.where(p != 0.0, 1.0, 0.0).astype(BF16)
        prob = jnp.sum(jnp.abs(p), axis=1, keepdims=True)
        y_send[z, :, 0:lanes] = dot(one, xs[...]).astype(BF16)
        y_send[z, :, lanes : lanes + 128] = jnp.broadcast_to(prob, (ROWS, 128)).astype(BF16)
        for o in (1, 3, 2):
            y_copy(z, o).start()
        mine = pl.ds(pl.multiple_of(y * CAP, CAP), CAP)
        rows[3 * z, mine, :] = y_send[z, mine, :]

    right, left = at(y, zh, (x + 1) % 4), at(y, zh, (x + 3) % 4)
    half = ROWS // 2

    def x_copy(i):
        src, dst, lo, n, to = (
            (0, 1, 0, ROWS, right),
            (0, 2, 0, ROWS, left),
            (3, 4, 0, ROWS, right),
            (3, 5, 0, ROWS, left),
            (1, 7, 0, half, right),
            (2, 7, half, half, left),
            (4, 6, 0, half, right),
            (5, 6, half, half, left),
        )[i]
        part = pl.ds(lo, n)
        return remote(rows.at[src, part], rows.at[dst, part], x_s.at[i], x_r.at[i], to)

    def pair_copy(d, k):
        return remote(
            pair_send.at[k % 2, d],
            pair_recv.at[d, pl.ds(k * ROWS, ROWS)],
            pair_s.at[d, k],
            pair_r.at[d, k],
            partner,
        )

    def sub_rows(s):
        return pl.ds(pl.multiple_of(s * SUB, SUB), SUB)

    def line_copy(d, s):
        part = line.at[d, sub_rows(s)]
        return remote(part, part, line_s.at[d, s], line_r.at[d, s], below if d == 0 else above)

    def cast_copy(d, s):
        part = hid.at[2 * d + core, sub_rows(s)]
        return remote(part, part, cast_s.at[d, s], cast_r.at[d, s], above if d == 0 else below)

    def core_copy(d, s):
        part = hid.at[2 * d + core, sub_rows(s)]
        return remote(part, part, core_s.at[d, s], core_r.at[d, s], partner)

    def core_wait(d, s):
        part = hid.at[2 * d + 1 - core, sub_rows(s)]
        remote(part, part, core_s.at[d, s], core_r.at[d, s], partner).wait_recv()

    def project(k):
        @pl.when(k >= 2)
        def _():
            for d in range(2):
                pair_copy(d, k - 2).wait_send()

        for d in range(2):
            for mine in (False, True):
                q = 2 * d + (core if mine else 1 - core)
                up = dot(rows[k, :, 0:width], w_in[q])
                back = dot_nt(
                    rows[k, :, width:lanes],
                    w_out[pl.ds(pl.multiple_of(q * QUARTER, QUARTER), QUARTER), :],
                )
                if mine:
                    part = pl.ds(pl.multiple_of(k * ROWS, ROWS), ROWS)
                    own[d, part, 0 : 2 * QUARTER] = up
                    own[d, part, 2 * QUARTER : 3 * QUARTER] = back
                else:
                    pair_send[k % 2, d, :, 0 : 2 * QUARTER] = up
                    pair_send[k % 2, d, :, 2 * QUARTER : 3 * QUARTER] = back
                    pair_copy(d, k).start()

    def reduce(d, s):
        place = 3 - zl if d == 0 else zl

        @pl.when((s >= 0) & (s < NSUB))
        def _():
            @pl.when(s % PER == 0)
            def _():
                pair_copy(d, s // PER).wait_recv()

            part = sub_rows(s)

            @pl.when(place == 0)
            def _():
                line[d, part, :] = (own[d, part, :] + pair_recv[d, part, :]).astype(BF16)
                line_copy(d, s).start()

            @pl.when((place == 1) | (place == 2))
            def _():
                line_copy(d, s).wait_recv()
                total = own[d, part, :] + pair_recv[d, part, :] + line[d, part, :].astype(F32)
                line[d, part, :] = total.astype(BF16)
                line_copy(d, s).start()

            @pl.when(place == 3)
            def _():
                line_copy(d, s).wait_recv()
                total = own[d, part, :] + pair_recv[d, part, :] + line[d, part, :].astype(F32)
                gate = total[:, 0:QUARTER]
                up = total[:, QUARTER : 2 * QUARTER]
                back = total[:, 2 * QUARTER : 3 * QUARTER]
                inside = pl.ds(pl.multiple_of((s % PER) * SUB, SUB), SUB)
                prob = rows[s // PER, inside, lanes : lanes + 128].astype(F32)
                prob = jnp.concatenate([prob, prob], axis=1)
                sig = jax.nn.sigmoid(gate)
                hidden = (gate * sig * up).astype(BF16)
                grad = prob * back
                q = 2 * d + core
                hid[q, part, 0:QUARTER] = hidden
                hid[q, part, QUARTER : 2 * QUARTER] = (
                    grad * up * sig * (1.0 + gate * (1.0 - sig))
                ).astype(BF16)
                hid[q, part, 2 * QUARTER : 3 * QUARTER] = (grad * gate * sig).astype(BF16)
                term = jnp.sum(hidden.astype(F32) * back, axis=1, keepdims=True)
                hid[q, part, 3 * QUARTER : 3 * QUARTER + 128] = two_parts(term, SUB)
                cast_copy(d, s).start()
                core_copy(d, s).start()

    def two_parts(term, n):
        high = term.astype(BF16).astype(F32)
        lane = lax.broadcasted_iota(jnp.int32, (n, 128), 1)
        return jnp.where(lane < 64, high, term - high).astype(BF16)

    def spread(d, s):
        place = 3 - zl if d == 0 else zl

        @pl.when((s >= 0) & (s < NSUB) & (place < 3))
        def _():
            cast_copy(d, s).wait_recv()

            @pl.when(place > 0)
            def _():
                cast_copy(d, s).start()

            core_copy(d, s).start()

    def chunk_place(k):
        zi = jnp.where((k >= 3) & (k < 7), 1, 0)
        step = jnp.where(
            (k == 0) | (k == 3), 0, jnp.where((k == 1) | (k == 4), 3, jnp.where((k == 2) | (k == 5), 1, 2))
        )
        return zi, step

    def ret_copy(k, o):
        zi, step = chunk_place(k)
        to_y = (y + o) % 4
        return remote(
            ret_send.at[k % 2, pl.ds(to_y * CAP, CAP)],
            ret_recv.at[zi, here],
            ret_s.at[k, o],
            ret_r.at[zi, here],
            at(to_y, zh, (x + step) % 4),
        )

    def ret_wait(zi, o):
        source = (here + o) % 16
        remote(
            ret_send.at[0, pl.ds(0, CAP)],
            ret_recv.at[zi, source],
            ret_s.at[0, 0],
            ret_r.at[zi, source],
            plane(source),
        ).wait_recv()

    def ret_done(k):
        zi, step = chunk_place(k)

        @pl.when(step != 0)
        def _():
            ret_copy(k, 0).wait_send()

        for o in (1, 2, 3):
            ret_copy(k, o).wait_send()

    def back(k):
        for d in range(2):
            for i in range(PER):
                core_wait(d, k * PER + i)

        @pl.when(k >= 2)
        def _():
            ret_done(k - 2)

        part = pl.ds(pl.multiple_of(k * ROWS, ROWS), ROWS)
        total = dot_nt(hid[0, part, QUARTER : 3 * QUARTER], w_in[0])
        term = hid[0, part, 3 * QUARTER : 3 * QUARTER + 128].astype(F32)
        for q in range(1, 4):
            total += dot_nt(hid[q, part, QUARTER : 3 * QUARTER], w_in[q])
            term += hid[q, part, 3 * QUARTER : 3 * QUARTER + 128].astype(F32)
        ret_send[k % 2, :, 0:width] = total.astype(BF16)
        term = term[:, 0:1] + term[:, 64:65]
        ret_send[k % 2, :, width : width + 128] = two_parts(term, ROWS)
        zi, step = chunk_place(k)
        for o in (2, 1, 3):
            ret_copy(k, o).start()

        @pl.when(step != 0)
        def _():
            ret_copy(k, 0).start()

        @pl.when(step == 0)
        def _():
            mine = pl.ds(pl.multiple_of(y * CAP, CAP), CAP)
            ret_recv[zi, here] = ret_send[k % 2, mine, :]

    def weights(j):
        two = pl.ds(2 * j, 2)
        turned[...] = rows[two, :, 0:width].reshape(2 * ROWS, width).T
        prob = rows[two, :, lanes : lanes + 128].reshape(2 * ROWS, 128).astype(F32)
        grads = rows[two, :, width:lanes].reshape(2 * ROWS, width).astype(F32)
        scaled = (grads * jnp.concatenate([prob] * (width // 128), axis=1)).astype(BF16)
        part = pl.ds(pl.multiple_of(2 * j * ROWS, 2 * ROWS), 2 * ROWS)

        def one(q, _):
            acc_in[q] += dot(turned[...], hid[q, part, QUARTER : 3 * QUARTER])
            acc_out[q] += dot_tn(hid[q, part, 0:QUARTER], scaled)
            return 0

        lax.fori_loop(0, 4, one, 0)

    choose(0, x_ref, p_ref)
    acc_in[...] = jnp.zeros_like(acc_in)
    acc_out[...] = jnp.zeros_like(acc_out)
    for o in (1, 3, 2):
        y_wait(0, o)
    x_copy(0).start()
    x_copy(1).start()
    for copy in w_copies:
        copy.wait()
    project(0)

    up_end = 6 * LAG

    def tick(t, carry):
        for d in range(2):
            place = 3 - zl if d == 0 else zl
            spread(d, t - 3 * LAG - LAG * (3 - place))
        for d in range(2):
            place = 3 - zl if d == 0 else zl
            reduce(d, t - LAG * place)

        @pl.when(t == 1)
        def _():
            for copy in raw:
                copy.wait_recv()
            choose(1, x_other, p_other)

        @pl.when(((t + 1) % PER == 0) & (t + 1 < NSUB))
        def _():
            k = (t + 1) // PER

            @pl.when(k == 1)
            def _():
                x_copy(0).wait_recv()
                x_copy(4).start()
                for o in (1, 3, 2):
                    y_wait(1, o)
                x_copy(2).start()
                x_copy(3).start()

            @pl.when(k == 2)
            def _():
                x_copy(1).wait_recv()
                x_copy(5).start()

            @pl.when(k == 4)
            def _():
                x_copy(2).wait_recv()
                x_copy(6).start()

            @pl.when(k == 5)
            def _():
                x_copy(3).wait_recv()
                x_copy(7).start()

            @pl.when(k == 6)
            def _():
                x_copy(6).wait_recv()
                x_copy(7).wait_recv()

            @pl.when(k == 7)
            def _():
                x_copy(4).wait_recv()
                x_copy(5).wait_recv()

            project(k)

        @pl.when((t >= up_end + PER) & ((t - up_end) % PER == 0))
        def _():
            k = (t - up_end) // PER - 1
            back(k)

            @pl.when(k % 2 == 1)
            def _():
                weights(k // 2)

        return carry

    lax.fori_loop(0, NSUB + up_end + 1, tick, 0)

    for q in range(4):
        cols = pl.ds(q * QUARTER, QUARTER)
        out_g[:, cols] = acc_in[q, :, 0:QUARTER].astype(BF16)
        out_u[:, cols] = acc_in[q, :, QUARTER : 2 * QUARTER].astype(BF16)
        out_d[cols, :] = acc_out[q].astype(BF16)

    lane = lax.broadcasted_iota(jnp.int32, (x_ref.shape[0], 128), 1)

    def collect(zi, ps):
        for o in range(1, 16):
            ret_wait(zi, o)
        got = ret_recv[zi].reshape(16 * CAP, width + 128)
        p = ps[...].astype(F32)
        first = jnp.where(p > 0.0, 1.0, 0.0).astype(BF16)
        second = jnp.where(p < 0.0, 1.0, 0.0).astype(BF16)
        for i in range(16):
            part = pl.ds(i * CAP, CAP)
            e = (i // 4) * CAP
            pick[0, part, :] = first[e : e + CAP, :]
            pick[1, part, :] = second[e : e + CAP, :]
        both = pick[0] + pick[1]
        total = dot_tn(both, got[:, 0:width])
        terms = [dot_tn(pick[i], got[:, width : width + 128]) for i in range(2)]
        terms = [t[:, 0:1] + t[:, 64:65] for t in terms]
        highs = [t.astype(BF16).astype(F32) for t in terms]
        packed = jnp.where(
            lane < 64,
            jnp.where(lane < 32, highs[0], terms[0] - highs[0]),
            jnp.where(lane < 96, highs[1], terms[1] - highs[1]),
        )
        return total, packed

    total, packed = collect(1, p_other)
    z_send[:, 0:width] = total.astype(BF16)
    z_send[:, width : width + 128] = packed.astype(BF16)
    last = remote(z_send, z_recv, last_s.at[0], last_r.at[0], other_z)
    last.start()
    total, packed = collect(0, p_ref)
    last.wait_recv()
    out_x[...] = (total + z_recv[:, 0:width].astype(F32)).astype(BF16)
    out_p[...] = packed + z_recv[:, width : width + 128].astype(F32)

    last.wait_send()
    for copy in raw:
        copy.wait_send()
    for z in range(2):
        for o in (1, 2, 3):
            y_copy(z, o).wait_send()
    for i in range(8):
        x_copy(i).wait_send()
    for k in (CHUNKS - 2, CHUNKS - 1):
        for d in range(2):
            pair_copy(d, k).wait_send()
        ret_done(k)

    def drain(s, carry):
        for d in range(2):
            place = 3 - zl if d == 0 else zl

            @pl.when(place < 3)
            def _():
                line_copy(d, s).wait_send()

            @pl.when(place > 0)
            def _():
                cast_copy(d, s).wait_send()

            core_copy(d, s).wait_send()
        return carry

    lax.fori_loop(0, NSUB, drain, 0)


def layer(xs, ps, gate_weight, up_weight, down_weight):
    width, hid = gate_weight.shape
    tok = xs.shape[0]
    total = CHUNKS * ROWS
    vm = pltpu.VMEM
    dma = pltpu.SemaphoreType.DMA
    inner = pl.BlockSpec(memory_space=pltpu.VMEM)
    outer = pl.BlockSpec(memory_space=pl.ANY)
    message = 3 * QUARTER
    return pl.pallas_call(
        functools.partial(kernel, width),
        out_shape=(
            jax.ShapeDtypeStruct((tok, width), BF16),
            jax.ShapeDtypeStruct((tok, 128), F32),
            jax.ShapeDtypeStruct((width, hid), BF16),
            jax.ShapeDtypeStruct((width, hid), BF16),
            jax.ShapeDtypeStruct((hid, width), BF16),
        ),
        in_specs=[inner, inner, outer, outer, outer],
        out_specs=(inner,) * 5,
        scratch_shapes=[
            vm((tok, 2 * width), BF16),
            vm((ROWS, tok), BF16),
            vm((CHUNKS, ROWS, 2 * width + 128), BF16),
            vm((2, ROWS, 2 * width + 128), BF16),
            vm((4, width, 2 * QUARTER), BF16),
            vm((hid, width), BF16),
            vm((2, total, message), F32),
            vm((2, 2, ROWS, message), F32),
            vm((2, total, message), F32),
            vm((2, total, message), BF16),
            vm((4, total, message + 128), BF16),
            vm((2, ROWS, width + 128), BF16),
            vm((2, 16, CAP, width + 128), BF16),
            vm((2, 16 * CAP, tok), BF16),
            vm((tok, width + 128), BF16),
            vm((tok, width + 128), BF16),
            vm((4, width, 2 * QUARTER), F32),
            vm((4, QUARTER, width), F32),
            vm((width, 2 * ROWS), BF16),
            dma((9,)),
            dma((2,)),
            dma((2,)),
            dma((2, 4)),
            dma((2, 4)),
            dma((8,)),
            dma((8,)),
            dma((2, CHUNKS)),
            dma((2, CHUNKS)),
            dma((2, NSUB)),
            dma((2, NSUB)),
            dma((2, NSUB)),
            dma((2, NSUB)),
            dma((2, NSUB)),
            dma((2, NSUB)),
            dma((CHUNKS, 4)),
            dma((2, 16)),
            dma((1,)),
            dma((1,)),
        ],
        compiler_params=pltpu.CompilerParams(
            collective_id=0, has_side_effects=True, vmem_limit_bytes=67043328
        ),
    )(xs, ps, gate_weight, up_weight, down_weight)


def slot_probs(expert_ids, gate_prob):
    labels = expert_ids.reshape(-1)
    onehot = (labels[:, None] == jnp.arange(EXPERTS, dtype=jnp.int32)[None, :]).astype(jnp.int32)
    before = jnp.cumsum(onehot, axis=0) - onehot
    places = jnp.sum(before * onehot, axis=1)
    codes = (labels * CAP + places).reshape(-1, 2)
    slots = jnp.arange(ROWS, dtype=jnp.int32)[:, None]
    zero = jnp.zeros((), BF16)
    first = jnp.where(slots == codes[None, :, 0], gate_prob[None, :, 0], zero)
    second = jnp.where(slots == codes[None, :, 1], gate_prob[None, :, 1], zero)
    return first - second


def body(tokens, out_grad, expert_ids, gate_prob, gate_weight, up_weight, down_weight):
    xs = jnp.concatenate([tokens, out_grad], axis=1)
    ps = slot_probs(expert_ids, gate_prob)
    input_grad, terms, gate_grad, up_grad, down_grad = layer(xs, ps, gate_weight, up_weight, down_weight)
    prob_grad = jnp.stack([terms[:, 0] + terms[:, 32], terms[:, 64] + terms[:, 96]], axis=1)
    return (input_grad, prob_grad, gate_grad, up_grad, down_grad)


def solution(mesh):
    return jax.shard_map(
        body,
        mesh=mesh,
        in_specs=(
            P("dp", "tensor"),
            P("dp", "tensor"),
            P("dp", None),
            P("dp", None),
            P("tensor", "dp"),
            P("tensor", "dp"),
            P("dp", "tensor"),
        ),
        out_specs=(
            P("dp", "tensor"),
            P("dp", None),
            P("tensor", "dp"),
            P("tensor", "dp"),
            P("dp", "tensor"),
        ),
        check_vma=False,
    )
```

time: 431 us -> 152 us (0.35)
  waiting for transfers between devices: 271 us -> 0 us
  Pallas kernels: 0 us -> 137 us
  blocking collectives: 45.4 us -> 0 us
  starting transfers between devices: 42.2 us -> 0 us
  matrix products: 37.4 us -> 0 us
  between operations: 14.2 us -> 0.68 us
  other arithmetic: 11.7 us -> 4.87 us
    pallas_call x0 -> x1, Pallas kernels: none -> 137 us  [layer(): pl.pallas_call(functools.partial(kernel, width), out_shape=(jax.ShapeDtyp...]
    reduce_scatter x1 -> x0, waiting for transfers between devices: 136 us -> none  [sent_together(): result = lax.psum_scatter(both, axis, scatter_dimension=dim, tiled=True)]
    all_to_all x4 -> x0, waiting for transfers between devices: 96.6 us -> none  [the longest x1 59.4 us: body(): lax.all_to_all(input_part.reshape(dp_count, CAP, part_width), 'dp', split...]
    all_to_all x4 -> x0, starting transfers between devices: 42.1 us -> none  [the longest x1 14.6 us: body(): lax.all_to_all(jnp.repeat(send_rows, group_size, axis=0), 'dp', split_axi...]
    all_gather x1 -> x0, waiting for transfers between devices: 38.2 us -> none  [side_by_side(): lax.all_gather(both, axis, axis=dim, tiled=True)]
    dot_general x13 -> x0, matrix products: 37.4 us -> none  [the longest x3 14.4 us: inner_rows(): lax.dot_general(left, right, (((0,), (0,)), ((), ())), preferred_element_...]
    psum x1 -> x0, blocking collectives: 25.4 us -> none  [body(): lax.psum(jnp.sum(hidden_share.astype(jnp.float32) * back_hidden, axis=1),...]
    all_to_all x1 -> x0, blocking collectives: 20.1 us -> none  [body(): lax.all_to_all(jnp.repeat(send_probs, group_size, axis=0), 'dp', split_ax...]
  transfers between devices with their start and end apart: 6 -> 0, of which waited for: 5 -> 0; matrix products, arithmetic and copies ran while one was open for 8% -> 0% of each run, Pallas kernels for 0% -> 0%
where the time goes in v1:
time: 152 us
  Pallas kernels  137 us (90%)
  local copies, waits for them, and re-layouts  9.4 us (6%)
  other arithmetic  4.87 us (3%)
    pallas_call x1, Pallas kernels, layer(): pl.pallas_call(functools.partial(kernel, width), out_shape=(jax.ShapeDtyp...  137 us
    unnamed x9, local copies, waits for them, and re-layouts  8.19 us

profile of v1, /device:TPU:1, one launch (start us, length us, event | category | flops | bytes accessed | tf_op | source)
XLA Modules:
  0.0 152.0 jit_solution(2791271574065988886)
XLA Ops:
  0.6 0.7 slice_bitcast_fusion.2
  1.4 0.8 copy.25
  2.1 0.1 eq.46
  2.3 0.1 fusion.2
  2.3 0.1 reduce_window_sum.11
  2.5 0.2 select_reduce_fusion
  2.7 0.1 reduce_sum.12
  2.8 0.1 copy.26
  2.9 0.7 multiply_add_fusion
  3.6 0.6 fusion.3.p_ref
  4.2 1.6 %pad_maximum_fusion.x_ref = bf16[48,1536]{1,0:T(8,128)(2,1)} fusion(bf16[48,768]{1,0:T(8,128)(2,1)} %param.8, bf16[48,768]{1,0:T(8,128)(2,1)} %param.7), kind=kLoop, calls=%fused_computation | loop fusion | flops 294912 | bytes 294912 | tf_op jit(solution)/shard_map/concatenate | solution.py:623
  5.8 137.1 %shard_map.110 = (bf16[48,768]{1,0:T(8,128)(2,1)}, f32[48,128]{1,0:T(8,128)}, bf16[768,1024]{1,0:T(8,128)(2,1)}, bf16[768,1024]{1,0:T(8,128)(2,1)}, bf16[1024,768]{1,0:T(8,128)(2,1)}) custom-call(bf16[48,1536]{1,0:T(8,128)(2,1)} %pad_maximum_fusion.x_ref, bf16[128,48]{1,0:T(8,128)(2,1)} %fusion.3.p_ref, bf16[768,1024]{1,0:T(8,128)(2,1)} %wg_ref.1, ...), custom_call_target="tpu_custom_call" | custom-call | tf_op jit(solution)/shard_map/pallas_call | solution.py:552
  142.9 1.0 slice_add_fusion.1
  143.9 0.1 copy.27
  143.9 0.1 copy.28
  144.0 0.6 pad_maximum_fusion.1
  144.6 1.5 %copy.33 = bf16[48,768]{1,0:T(8,128)(2,1)} copy(bf16[48,768]{1,0:T(8,128)(2,1)} %get-tuple-element.36) | data formatting | bytes 147456
  146.1 0.0 copy-start.1
  146.1 2.8 %copy.34 = bf16[768,1024]{1,0:T(8,128)(2,1)} copy(bf16[768,1024]{1,0:T(8,128)(2,1)} %get-tuple-element.38) | data formatting | bytes 3145728
  148.9 0.0 copy-done.1
  148.9 0.0 copy-start
  148.9 1.1 copy.35
  150.1 0.8 copy-done
  150.9 1.1 copy.36
  (1 shorter events, 0.0 us)
Async XLA Ops:
  146.1 2.8 %copy-start.1 = (bf16[768,1024]{1,0:T(8,128)(2,1)S(1)}, bf16[768,1024]{1,0:T(8,128)(2,1)}, u32[]{:S(2)}) copy-start(bf16[768,1024]{1,0:T(8,128)(2,1)} %get-tuple-element.39) | copy-start | bytes 4718596
  148.9 2.0 %copy-start = (bf16[1024,768]{1,0:T(8,128)(2,1)S(1)}, bf16[1024,768]{1,0:T(8,128)(2,1)}, u32[]{:S(2)}) copy-start(bf16[1024,768]{1,0:T(8,128)(2,1)} %get-tuple-element.40) | copy-start | bytes 4718596

commit v2 on v1

--- a/solution.py
+++ b/solution.py
@@ -35,8 +35,10 @@
 
 def kernel(
     width,
-    x_ref,
-    p_ref,
+    tok_ref,
+    grad_ref,
+    ids_ref,
+    prob_ref,
     wg_ref,
     wu_ref,
     wd_ref,
@@ -46,7 +48,9 @@
     out_u,
     out_d,
     x_other,
-    p_other,
+    ids_other,
+    prob_other,
+    p_all,
     rows,
     y_send,
     w_in,
@@ -61,6 +65,8 @@
     pick,
     z_send,
     z_recv,
+    t_send,
+    t_recv,
     acc_in,
     acc_out,
     turned,
@@ -130,14 +136,12 @@
 
     pl.semaphore_signal(barrier, inc=1, device_id=above, device_id_type=MESH)
     pl.semaphore_signal(barrier, inc=1, device_id=below, device_id_type=MESH)
-    pl.semaphore_wait(barrier, 19)
-
     raw = [
-        remote(x_ref, x_other, z_s.at[0], z_r.at[0], other_z),
-        remote(p_ref, p_other, z_s.at[1], z_r.at[1], other_z),
+        remote(ids_ref, ids_other, z_s.at[0], z_r.at[0], other_z),
+        remote(prob_ref, prob_other, z_s.at[1], z_r.at[1], other_z),
+        remote(tok_ref, x_other.at[0], z_s.at[2], z_r.at[2], other_z),
+        remote(grad_ref, x_other.at[1], z_s.at[3], z_r.at[3], other_z),
     ]
-    for copy in raw:
-        copy.start()
 
     def y_copy(z, o):
         to = (y + o) % 4
@@ -159,12 +163,30 @@
             at(source, zh, x),
         ).wait_recv()
 
-    def choose(z, xs, ps):
-        p = ps[...].astype(F32)
+    def choose(z, toks, grads, ids, probs):
+        count = ids.shape[1]
+        named = lax.broadcasted_iota(jnp.int32, (8, count), 0)
+        member = jnp.where((named == ids[0:1, :]) | (named == ids[1:2, :]), 1.0, 0.0)
+        earlier = jnp.where(
+            lax.broadcasted_iota(jnp.int32, (count, count), 0)
+            < lax.broadcasted_iota(jnp.int32, (count, count), 1),
+            1.0,
+            0.0,
+        )
+        before = dot(member.astype(BF16), earlier.astype(BF16))
+        slot = lax.broadcasted_iota(jnp.int32, (CAP, count), 0).astype(F32)
+        for e in range(EXPERTS):
+            value = jnp.where(ids[0:1, :] == e, probs[0:1, :], -probs[1:2, :])
+            value = jnp.where(member[e : e + 1, :] > 0.0, value, 0.0)
+            p_all[z, e * CAP : (e + 1) * CAP, :] = jnp.where(slot == before[e : e + 1, :], value, 0.0)
+        p = p_all[z]
         one = jnp.where(p != 0.0, 1.0, 0.0).astype(BF16)
         prob = jnp.sum(jnp.abs(p), axis=1, keepdims=True)
-        y_send[z, :, 0:lanes] = dot(one, xs[...]).astype(BF16)
+        y_send[z, :, 0:width] = dot(one, toks).astype(BF16)
+        y_send[z, :, width:lanes] = dot(one, grads).astype(BF16)
         y_send[z, :, lanes : lanes + 128] = jnp.broadcast_to(prob, (ROWS, 128)).astype(BF16)
+
+    def deal(z):
         for o in (1, 3, 2):
             y_copy(z, o).start()
         mine = pl.ds(pl.multiple_of(y * CAP, CAP), CAP)
@@ -381,15 +403,35 @@
         part = pl.ds(pl.multiple_of(2 * j * ROWS, 2 * ROWS), 2 * ROWS)
 
         def one(q, _):
-            acc_in[q] += dot(turned[...], hid[q, part, QUARTER : 3 * QUARTER])
-            acc_out[q] += dot_tn(hid[q, part, 0:QUARTER], scaled)
+            up = dot(turned[...], hid[q, part, QUARTER : 3 * QUARTER])
+            down = dot_tn(hid[q, part, 0:QUARTER], scaled)
+
+            @pl.when(j == 0)
+            def _():
+                acc_in[q] = up
+                acc_out[q] = down
+
+            @pl.when((j > 0) & (j < CHUNKS // 2 - 1))
+            def _():
+                acc_in[q] += up
+                acc_out[q] += down
+
+            @pl.when(j == CHUNKS // 2 - 1)
+            def _():
+                cols = pl.ds(pl.multiple_of(q * QUARTER, QUARTER), QUARTER)
+                out_g[:, cols] = (acc_in[q, :, 0:QUARTER] + up[:, 0:QUARTER]).astype(BF16)
+                out_u[:, cols] = (acc_in[q, :, QUARTER : 2 * QUARTER] + up[:, QUARTER : 2 * QUARTER]).astype(BF16)
+                out_d[cols, :] = (acc_out[q] + down).astype(BF16)
+
             return 0
 
         lax.fori_loop(0, 4, one, 0)
 
-    choose(0, x_ref, p_ref)
-    acc_in[...] = jnp.zeros_like(acc_in)
-    acc_out[...] = jnp.zeros_like(acc_out)
+    choose(0, tok_ref[...], grad_ref[...], ids_ref[...], prob_ref[...].astype(F32))
+    pl.semaphore_wait(barrier, 19)
+    deal(0)
+    for copy in raw:
+        copy.start()
     for o in (1, 3, 2):
         y_wait(0, o)
     x_copy(0).start()
@@ -398,6 +440,27 @@
         copy.wait()
     project(0)
 
+    def collect(zi):
+        for o in range(1, 16):
+            ret_wait(zi, o)
+        got = ret_recv[zi].reshape(16 * CAP, width + 128)
+        p = p_all[zi]
+        first = jnp.where(p > 0.0, 1.0, 0.0).astype(BF16)
+        second = jnp.where(p < 0.0, 1.0, 0.0).astype(BF16)
+        for i in range(16):
+            part = pl.ds(i * CAP, CAP)
+            e = (i // 4) * CAP
+            pick[0, part, :] = first[e : e + CAP, :]
+            pick[1, part, :] = second[e : e + CAP, :]
+        terms = [dot_tn(got[:, width : width + 128], pick[i]) for i in range(2)]
+        terms = [t[0:1, :] + t[64:65, :] for t in terms]
+        return dot_tn(pick[0] + pick[1], got[:, 0:width]), jnp.concatenate(terms, axis=0)
+
+    last = [
+        remote(z_send, z_recv, last_s.at[0], last_r.at[0], other_z),
+        remote(t_send, t_recv, last_s.at[1], last_r.at[1], other_z),
+    ]
+
     up_end = 6 * LAG
 
     def tick(t, carry):
@@ -412,7 +475,8 @@
         def _():
             for copy in raw:
                 copy.wait_recv()
-            choose(1, x_other, p_other)
+            choose(1, x_other[0], x_other[1], ids_other[...], prob_other[...].astype(F32))
+            deal(1)
 
         @pl.when(((t + 1) % PER == 0) & (t + 1 < NSUB))
         def _():
@@ -459,6 +523,14 @@
             k = (t - up_end) // PER - 1
             back(k)
 
+            @pl.when(k == CHUNKS - 1)
+            def _():
+                grads, terms = collect(1)
+                z_send[...] = grads.astype(BF16)
+                t_send[...] = terms
+                for copy in last:
+                    copy.start()
+
             @pl.when(k % 2 == 1)
             def _():
                 weights(k // 2)
@@ -467,49 +539,14 @@
 
     lax.fori_loop(0, NSUB + up_end + 1, tick, 0)
 
-    for q in range(4):
-        cols = pl.ds(q * QUARTER, QUARTER)
-        out_g[:, cols] = acc_in[q, :, 0:QUARTER].astype(BF16)
-        out_u[:, cols] = acc_in[q, :, QUARTER : 2 * QUARTER].astype(BF16)
-        out_d[cols, :] = acc_out[q].astype(BF16)
-
-    lane = lax.broadcasted_iota(jnp.int32, (x_ref.shape[0], 128), 1)
-
-    def collect(zi, ps):
-        for o in range(1, 16):
-            ret_wait(zi, o)
-        got = ret_recv[zi].reshape(16 * CAP, width + 128)
-        p = ps[...].astype(F32)
-        first = jnp.where(p > 0.0, 1.0, 0.0).astype(BF16)
-        second = jnp.where(p < 0.0, 1.0, 0.0).astype(BF16)
-        for i in range(16):
-            part = pl.ds(i * CAP, CAP)
-            e = (i // 4) * CAP
-            pick[0, part, :] = first[e : e + CAP, :]
-            pick[1, part, :] = second[e : e + CAP, :]
-        both = pick[0] + pick[1]
-        total = dot_tn(both, got[:, 0:width])
-        terms = [dot_tn(pick[i], got[:, width : width + 128]) for i in range(2)]
-        terms = [t[:, 0:1] + t[:, 64:65] for t in terms]
-        highs = [t.astype(BF16).astype(F32) for t in terms]
-        packed = jnp.where(
-            lane < 64,
-            jnp.where(lane < 32, highs[0], terms[0] - highs[0]),
-            jnp.where(lane < 96, highs[1], terms[1] - highs[1]),
-        )
-        return total, packed
-
-    total, packed = collect(1, p_other)
-    z_send[:, 0:width] = total.astype(BF16)
-    z_send[:, width : width + 128] = packed.astype(BF16)
-    last = remote(z_send, z_recv, last_s.at[0], last_r.at[0], other_z)
-    last.start()
-    total, packed = collect(0, p_ref)
-    last.wait_recv()
-    out_x[...] = (total + z_recv[:, 0:width].astype(F32)).astype(BF16)
-    out_p[...] = packed + z_recv[:, width : width + 128].astype(F32)
-
-    last.wait_send()
+    grads, terms = collect(0)
+    for copy in last:
+        copy.wait_recv()
+    out_x[...] = (grads + z_recv[...].astype(F32)).astype(BF16)
+    out_p[...] = terms + t_recv[...]
+
+    for copy in last:
+        copy.wait_send()
     for copy in raw:
         copy.wait_send()
     for z in range(2):
@@ -540,9 +577,9 @@
     lax.fori_loop(0, NSUB, drain, 0)
 
 
-def layer(xs, ps, gate_weight, up_weight, down_weight):
+def layer(tokens, out_grad, ids, probs, gate_weight, up_weight, down_weight):
     width, hid = gate_weight.shape
-    tok = xs.shape[0]
+    tok = tokens.shape[0]
     total = CHUNKS * ROWS
     vm = pltpu.VMEM
     dma = pltpu.SemaphoreType.DMA
@@ -552,17 +589,19 @@
     return pl.pallas_call(
         functools.partial(kernel, width),
         out_shape=(
-            jax.ShapeDtypeStruct((tok, width), BF16),
-            jax.ShapeDtypeStruct((tok, 128), F32),
-            jax.ShapeDtypeStruct((width, hid), BF16),
-            jax.ShapeDtypeStruct((width, hid), BF16),
-            jax.ShapeDtypeStruct((hid, width), BF16),
+            vm((tok, width), BF16),
+            vm((2, tok), F32),
+            vm((width, hid), BF16),
+            vm((width, hid), BF16),
+            vm((hid, width), BF16),
         ),
-        in_specs=[inner, inner, outer, outer, outer],
+        in_specs=[inner, inner, inner, inner, outer, outer, outer],
         out_specs=(inner,) * 5,
         scratch_shapes=[
-            vm((tok, 2 * width), BF16),
-            vm((ROWS, tok), BF16),
+            vm((2, tok, width), BF16),
+            vm((2, tok), jnp.int32),
+            vm((2, tok), BF16),
+            vm((2, ROWS, tok), F32),
             vm((CHUNKS, ROWS, 2 * width + 128), BF16),
             vm((2, ROWS, 2 * width + 128), BF16),
             vm((4, width, 2 * QUARTER), BF16),
@@ -575,14 +614,16 @@
             vm((2, ROWS, width + 128), BF16),
             vm((2, 16, CAP, width + 128), BF16),
             vm((2, 16 * CAP, tok), BF16),
-            vm((tok, width + 128), BF16),
-            vm((tok, width + 128), BF16),
+            vm((tok, width), BF16),
+            vm((tok, width), BF16),
+            vm((2, tok), F32),
+            vm((2, tok), F32),
             vm((4, width, 2 * QUARTER), F32),
             vm((4, QUARTER, width), F32),
             vm((width, 2 * ROWS), BF16),
             dma((9,)),
-            dma((2,)),
-            dma((2,)),
+            dma((4,)),
+            dma((4,)),
             dma((2, 4)),
             dma((2, 4)),
             dma((8,)),
@@ -597,34 +638,20 @@
             dma((2, NSUB)),
             dma((CHUNKS, 4)),
             dma((2, 16)),
-            dma((1,)),
-            dma((1,)),
+            dma((2,)),
+            dma((2,)),
         ],
         compiler_params=pltpu.CompilerParams(
-            collective_id=0, has_side_effects=True, vmem_limit_bytes=67043328
+            collective_id=0, has_side_effects=True, vmem_limit_bytes=55 * 1024 * 1024
         ),
-    )(xs, ps, gate_weight, up_weight, down_weight)
-
-
-def slot_probs(expert_ids, gate_prob):
-    labels = expert_ids.reshape(-1)
-    onehot = (labels[:, None] == jnp.arange(EXPERTS, dtype=jnp.int32)[None, :]).astype(jnp.int32)
-    before = jnp.cumsum(onehot, axis=0) - onehot
-    places = jnp.sum(before * onehot, axis=1)
-    codes = (labels * CAP + places).reshape(-1, 2)
-    slots = jnp.arange(ROWS, dtype=jnp.int32)[:, None]
-    zero = jnp.zeros((), BF16)
-    first = jnp.where(slots == codes[None, :, 0], gate_prob[None, :, 0], zero)
-    second = jnp.where(slots == codes[None, :, 1], gate_prob[None, :, 1], zero)
-    return first - second
+    )(tokens, out_grad, ids, probs, gate_weight, up_weight, down_weight)
 
 
 def body(tokens, out_grad, expert_ids, gate_prob, gate_weight, up_weight, down_weight):
-    xs = jnp.concatenate([tokens, out_grad], axis=1)
-    ps = slot_probs(expert_ids, gate_prob)
-    input_grad, terms, gate_grad, up_grad, down_grad = layer(xs, ps, gate_weight, up_weight, down_weight)
-    prob_grad = jnp.stack([terms[:, 0] + terms[:, 32], terms[:, 64] + terms[:, 96]], axis=1)
-    return (input_grad, prob_grad, gate_grad, up_grad, down_grad)
+    input_grad, terms, gate_grad, up_grad, down_grad = layer(
+        tokens, out_grad, expert_ids.T, gate_prob.T, gate_weight, up_weight, down_weight
+    )
+    return (input_grad, terms.T, gate_grad, up_grad, down_grad)
 
 
 def solution(mesh):

time: 152 us -> 140 us (0.921)
  other arithmetic: 4.87 us -> 0 us
  local copies, waits for them, and re-layouts: 9.4 us -> 4.62 us
  Pallas kernels: 137 us -> 135 us
    unnamed x9 -> x5, local copies, waits for them, and re-layouts: 8.19 us -> 4.62 us
    pallas_call x1, Pallas kernels: 137 us -> 135 us  [layer(): pl.pallas_call(functools.partial(kernel, width), out_shape=(vm((tok, widt...]
    add x2 -> x0, other arithmetic: 1.67 us -> none  [the longest x1 0.97 us: body(): terms[:, 0] + terms[:, 32]]
    concatenate x1 -> x0, other arithmetic: 1.59 us -> none  [body(): xs = jnp.concatenate([tokens, out_grad], axis=1)]
where the time goes in v2:
time: 140 us
  Pallas kernels  135 us (96%)
  local copies, waits for them, and re-layouts  4.62 us (3%)
    pallas_call x1, Pallas kernels, layer(): pl.pallas_call(functools.partial(kernel, width), out_shape=(vm((tok, widt...  135 us
    unnamed x5, local copies, waits for them, and re-layouts  4.62 us

profile of v2, /device:TPU:1, one launch (start us, length us, event | category | flops | bytes accessed | tf_op | source)
XLA Modules:
  0.0 140.2 jit_solution(16319053524644861137)
XLA Ops:
  0.6 134.9 %shard_map.110 = (bf16[48,768]{1,0:T(8,128)(2,1)S(1)}, f32[2,48]{1,0:T(2,128)S(1)}, bf16[768,1024]{1,0:T(8,128)(2,1)S(1)}, bf16[768,1024]{1,0:T(8,128)(2,1)S(1)}, bf16[1024,768]{1,0:T(8,128)(2,1)S(1)}) custom-call(bf16[48,768]{1,0:T(8,128)(2,1)} %tok_ref.1, bf16[48,768]{1,0:T(8,128)(2,1)} %grad_ref.1, s32[2,48]{1,0:T(2,128)} %bitcast.4, ...), custom_call_target="tpu_custom_call" | custom-call | tf_op jit(solution)/shard_map/pallas_call | solution.py:589
  135.5 0.6 copy.17
  136.2 0.6 copy.18
  136.7 1.1 copy.19
  137.9 1.1 copy.20
  139.0 1.1 copy.21

commit v3 on v2

--- a/solution.py
+++ b/solution.py
@@ -70,6 +70,10 @@
     acc_in,
     acc_out,
     turned,
+    scaled,
+    term_send,
+    term_recv,
+    term_all,
     w_sem,
     z_s,
     z_r,
@@ -77,6 +81,8 @@
     y_r,
     x_s,
     x_r,
+    far_s,
+    far_r,
     pair_s,
     pair_r,
     line_s,
@@ -89,6 +95,10 @@
     ret_r,
     last_s,
     last_r,
+    term_s,
+    term_r,
+    all_s,
+    all_r,
 ):
     dp = lax.axis_index("dp")
     tensor = lax.axis_index("tensor")
@@ -105,6 +115,7 @@
 
     other_z = at(y, 1 - zh, x)
     partner = (dp, zl * 2 + 1 - core)
+    root = (zl == 0) | (zl == 3)
     above = (dp, (tensor + 2) % 8)
     below = (dp, (tensor + 6) % 8)
 
@@ -132,10 +143,9 @@
     for o in range(1, 16):
         pl.semaphore_signal(barrier, inc=1, device_id=plane((here + o) % 16), device_id_type=MESH)
     pl.semaphore_signal(barrier, inc=1, device_id=other_z, device_id_type=MESH)
-    pl.semaphore_signal(barrier, inc=1, device_id=partner, device_id_type=MESH)
-
-    pl.semaphore_signal(barrier, inc=1, device_id=above, device_id_type=MESH)
-    pl.semaphore_signal(barrier, inc=1, device_id=below, device_id_type=MESH)
+    for o in range(1, 8):
+        pl.semaphore_signal(barrier, inc=1, device_id=(dp, (tensor + o) % 8), device_id_type=MESH)
+
     raw = [
         remote(ids_ref, ids_other, z_s.at[0], z_r.at[0], other_z),
         remote(prob_ref, prob_other, z_s.at[1], z_r.at[1], other_z),
@@ -143,25 +153,26 @@
         remote(grad_ref, x_other.at[1], z_s.at[3], z_r.at[3], other_z),
     ]
 
+    def offset(g):
+        return jnp.where(g == 2, 3, jnp.where(g == 3, 2, g))
+
+    def group(g):
+        return pl.ds(g * CAP, CAP)
+
     def y_copy(z, o):
         to = (y + o) % 4
+        g = (None, 2, 3, 1)[o]
         return remote(
             y_send.at[z, pl.ds(to * CAP, CAP)],
-            rows.at[3 * z, pl.ds(y * CAP, CAP)],
-            y_s.at[z, to],
-            y_r.at[z, y],
+            rows.at[2 * z, group(g)],
+            y_s.at[z, o],
+            y_r.at[z, g],
             at(to, zh, x),
         )
 
-    def y_wait(z, o):
-        source = (y + o) % 4
-        remote(
-            y_send.at[z, pl.ds(source * CAP, CAP)],
-            rows.at[3 * z, pl.ds(source * CAP, CAP)],
-            y_s.at[z, source],
-            y_r.at[z, source],
-            at(source, zh, x),
-        ).wait_recv()
+    def y_wait(z, g):
+        part = rows.at[2 * z, group(g)]
+        remote(part, part, y_s.at[z, 0], y_r.at[z, g], other_z).wait_recv()
 
     def choose(z, toks, grads, ids, probs):
         count = ids.shape[1]
@@ -189,25 +200,43 @@
     def deal(z):
         for o in (1, 3, 2):
             y_copy(z, o).start()
-        mine = pl.ds(pl.multiple_of(y * CAP, CAP), CAP)
-        rows[3 * z, mine, :] = y_send[z, mine, :]
+        rows[2 * z, 0:CAP, :] = y_send[z, pl.ds(pl.multiple_of(y * CAP, CAP), CAP), :]
+        for side in range(2):
+            x_copy(z, side, 0).start()
 
     right, left = at(y, zh, (x + 1) % 4), at(y, zh, (x + 3) % 4)
     half = ROWS // 2
 
-    def x_copy(i):
-        src, dst, lo, n, to = (
-            (0, 1, 0, ROWS, right),
-            (0, 2, 0, ROWS, left),
-            (3, 4, 0, ROWS, right),
-            (3, 5, 0, ROWS, left),
-            (1, 7, 0, half, right),
-            (2, 7, half, half, left),
-            (4, 6, 0, half, right),
-            (5, 6, half, half, left),
+    def x_copy(z, side, g):
+        dst = ((1, 7), (3, 4))[z][side]
+        return remote(
+            rows.at[2 * z, group(g)],
+            rows.at[dst, group(g)],
+            x_s.at[z, side, g],
+            x_r.at[z, side, g],
+            (right, left)[side],
+        )
+
+    def x_pass(z):
+        for g in (1, 2, 3):
+            y_wait(z, g)
+            for side in range(2):
+                x_copy(z, side, g).start()
+
+    def x_wait(z):
+        for side in range(2):
+            for g in range(4):
+                x_copy(z, side, g).wait_recv()
+
+    def far_copy(i):
+        src, dst, lo, to = (
+            (1, 6, 0, right),
+            (7, 6, half, left),
+            (3, 5, 0, right),
+            (4, 5, half, left),
         )[i]
-        part = pl.ds(lo, n)
-        return remote(rows.at[src, part], rows.at[dst, part], x_s.at[i], x_r.at[i], to)
+        part = pl.ds(lo, half)
+        return remote(rows.at[src, part], rows.at[dst, part], far_s.at[i], far_r.at[i], to)
 
     def pair_copy(d, k):
         return remote(
@@ -303,9 +332,30 @@
                 ).astype(BF16)
                 hid[q, part, 2 * QUARTER : 3 * QUARTER] = (grad * gate * sig).astype(BF16)
                 term = jnp.sum(hidden.astype(F32) * back, axis=1, keepdims=True)
-                hid[q, part, 3 * QUARTER : 3 * QUARTER + 128] = two_parts(term, SUB)
                 cast_copy(d, s).start()
                 core_copy(d, s).start()
+                term_send[s] = two_parts(term, SUB)
+                zi, step = chunk_place(s // PER)
+                self_too = (s % PER == 0) & (step == 0)
+
+                @pl.when(self_too)
+                def _():
+                    term_recv[zi, here] = term_send[s]
+
+                @pl.when(jnp.logical_not(self_too))
+                def _():
+                    term_copy(s).start()
+
+    def term_copy(s):
+        zi, step = chunk_place(s // PER)
+        to_y = (y + offset(s % PER)) % 4
+        return remote(
+            term_send.at[s],
+            term_recv.at[zi, here],
+            term_s.at[s],
+            term_r.at[zi, here],
+            at(to_y, zh, (x + step) % 4),
+        )
 
     def two_parts(term, n):
         high = term.astype(BF16).astype(F32)
@@ -326,19 +376,19 @@
             core_copy(d, s).start()
 
     def chunk_place(k):
-        zi = jnp.where((k >= 3) & (k < 7), 1, 0)
+        zi = jnp.where((k >= 2) & (k < 6), 1, 0)
         step = jnp.where(
-            (k == 0) | (k == 3), 0, jnp.where((k == 1) | (k == 4), 3, jnp.where((k == 2) | (k == 5), 1, 2))
+            (k == 0) | (k == 2), 0, jnp.where((k == 1) | (k == 3), 3, jnp.where((k == 4) | (k == 7), 1, 2))
         )
         return zi, step
 
-    def ret_copy(k, o):
+    def ret_copy(k, g):
         zi, step = chunk_place(k)
-        to_y = (y + o) % 4
+        to_y = (y + (0, 1, 3, 2)[g]) % 4
         return remote(
-            ret_send.at[k % 2, pl.ds(to_y * CAP, CAP)],
+            ret_send.at[k % 2, group(g)],
             ret_recv.at[zi, here],
-            ret_s.at[k, o],
+            ret_s.at[k, g],
             ret_r.at[zi, here],
             at(to_y, zh, (x + step) % 4),
         )
@@ -374,16 +424,12 @@
 
         part = pl.ds(pl.multiple_of(k * ROWS, ROWS), ROWS)
         total = dot_nt(hid[0, part, QUARTER : 3 * QUARTER], w_in[0])
-        term = hid[0, part, 3 * QUARTER : 3 * QUARTER + 128].astype(F32)
         for q in range(1, 4):
             total += dot_nt(hid[q, part, QUARTER : 3 * QUARTER], w_in[q])
-            term += hid[q, part, 3 * QUARTER : 3 * QUARTER + 128].astype(F32)
-        ret_send[k % 2, :, 0:width] = total.astype(BF16)
-        term = term[:, 0:1] + term[:, 64:65]
-        ret_send[k % 2, :, width : width + 128] = two_parts(term, ROWS)
+        ret_send[k % 2] = total.astype(BF16)
         zi, step = chunk_place(k)
-        for o in (2, 1, 3):
-            ret_copy(k, o).start()
+        for g in (3, 1, 2):
+            ret_copy(k, g).start()
 
         @pl.when(step != 0)
         def _():
@@ -391,59 +437,48 @@
 
         @pl.when(step == 0)
         def _():
-            mine = pl.ds(pl.multiple_of(y * CAP, CAP), CAP)
-            ret_recv[zi, here] = ret_send[k % 2, mine, :]
-
-    def weights(j):
+            ret_recv[zi, here] = ret_send[k % 2, 0:CAP, :]
+
+    def weights_in(j):
         two = pl.ds(2 * j, 2)
         turned[...] = rows[two, :, 0:width].reshape(2 * ROWS, width).T
         prob = rows[two, :, lanes : lanes + 128].reshape(2 * ROWS, 128).astype(F32)
         grads = rows[two, :, width:lanes].reshape(2 * ROWS, width).astype(F32)
-        scaled = (grads * jnp.concatenate([prob] * (width // 128), axis=1)).astype(BF16)
+        scaled[...] = (grads * jnp.concatenate([prob] * (width // 128), axis=1)).astype(BF16)
+
+    def weights(j, q):
         part = pl.ds(pl.multiple_of(2 * j * ROWS, 2 * ROWS), 2 * ROWS)
-
-        def one(q, _):
-            up = dot(turned[...], hid[q, part, QUARTER : 3 * QUARTER])
-            down = dot_tn(hid[q, part, 0:QUARTER], scaled)
-
-            @pl.when(j == 0)
-            def _():
-                acc_in[q] = up
-                acc_out[q] = down
-
-            @pl.when((j > 0) & (j < CHUNKS // 2 - 1))
-            def _():
-                acc_in[q] += up
-                acc_out[q] += down
-
-            @pl.when(j == CHUNKS // 2 - 1)
-            def _():
-                cols = pl.ds(pl.multiple_of(q * QUARTER, QUARTER), QUARTER)
-                out_g[:, cols] = (acc_in[q, :, 0:QUARTER] + up[:, 0:QUARTER]).astype(BF16)
-                out_u[:, cols] = (acc_in[q, :, QUARTER : 2 * QUARTER] + up[:, QUARTER : 2 * QUARTER]).astype(BF16)
-                out_d[cols, :] = (acc_out[q] + down).astype(BF16)
-
-            return 0
-
-        lax.fori_loop(0, 4, one, 0)
+        up = dot(turned[...], hid[q, part, QUARTER : 3 * QUARTER])
+        down = dot_tn(hid[q, part, 0:QUARTER], scaled[...])
+
+        @pl.when(j == 0)
+        def _():
+            acc_in[q] = up
+            acc_out[q] = down
+
+        @pl.when((j > 0) & (j < CHUNKS // 2 - 1))
+        def _():
+            acc_in[q] += up
+            acc_out[q] += down
+
+        @pl.when(j == CHUNKS // 2 - 1)
+        def _():
+            cols = pl.ds(pl.multiple_of(q * QUARTER, QUARTER), QUARTER)
+            out_g[:, cols] = (acc_in[q, :, 0:QUARTER] + up[:, 0:QUARTER]).astype(BF16)
+            out_u[:, cols] = (acc_in[q, :, QUARTER : 2 * QUARTER] + up[:, QUARTER : 2 * QUARTER]).astype(BF16)
+            out_d[cols, :] = (acc_out[q] + down).astype(BF16)
 
     choose(0, tok_ref[...], grad_ref[...], ids_ref[...], prob_ref[...].astype(F32))
-    pl.semaphore_wait(barrier, 19)
+    pl.semaphore_wait(barrier, 23)
     deal(0)
     for copy in raw:
         copy.start()
-    for o in (1, 3, 2):
-        y_wait(0, o)
-    x_copy(0).start()
-    x_copy(1).start()
+    x_pass(0)
     for copy in w_copies:
         copy.wait()
     project(0)
 
-    def collect(zi):
-        for o in range(1, 16):
-            ret_wait(zi, o)
-        got = ret_recv[zi].reshape(16 * CAP, width + 128)
+    def chosen(zi):
         p = p_all[zi]
         first = jnp.where(p > 0.0, 1.0, 0.0).astype(BF16)
         second = jnp.where(p < 0.0, 1.0, 0.0).astype(BF16)
@@ -452,14 +487,37 @@
             e = (i // 4) * CAP
             pick[0, part, :] = first[e : e + CAP, :]
             pick[1, part, :] = second[e : e + CAP, :]
-        terms = [dot_tn(got[:, width : width + 128], pick[i]) for i in range(2)]
+
+    def collect(zi):
+        for o in range(1, 16):
+            ret_wait(zi, o)
+        chosen(zi)
+        return dot_tn(pick[0] + pick[1], ret_recv[zi].reshape(16 * CAP, width))
+
+    def collect_terms(zi):
+        for o in range(1, 16):
+            source = (here + o) % 16
+            part = term_recv.at[zi, source]
+            remote(part, part, term_s.at[0], term_r.at[zi, source], plane(source)).wait_recv()
+        chosen(zi)
+        got = term_recv[zi].reshape(16 * CAP, 128)
+        terms = [dot_tn(got, pick[i]) for i in range(2)]
         terms = [t[0:1, :] + t[64:65, :] for t in terms]
-        return dot_tn(pick[0] + pick[1], got[:, 0:width]), jnp.concatenate(terms, axis=0)
-
-    last = [
-        remote(z_send, z_recv, last_s.at[0], last_r.at[0], other_z),
-        remote(t_send, t_recv, last_s.at[1], last_r.at[1], other_z),
-    ]
+        return jnp.concatenate(terms, axis=0)
+
+    slot = jnp.where(zl == 3, 2, 0) + core
+
+    def all_copy(o):
+        return remote(
+            term_all.at[slot],
+            term_all.at[slot],
+            all_s.at[o],
+            all_r.at[slot],
+            (dp, (tensor + o) % 8),
+        )
+
+    last = remote(z_send, z_recv, last_s.at[0], last_r.at[0], other_z)
+    last_term = remote(t_send, t_recv, last_s.at[1], last_r.at[1], other_z)
 
     up_end = 6 * LAG
 
@@ -478,82 +536,127 @@
             choose(1, x_other[0], x_other[1], ids_other[...], prob_other[...].astype(F32))
             deal(1)
 
+        @pl.when(t == PER + 1)
+        def _():
+            x_pass(1)
+
         @pl.when(((t + 1) % PER == 0) & (t + 1 < NSUB))
         def _():
             k = (t + 1) // PER
 
             @pl.when(k == 1)
             def _():
-                x_copy(0).wait_recv()
-                x_copy(4).start()
-                for o in (1, 3, 2):
-                    y_wait(1, o)
-                x_copy(2).start()
-                x_copy(3).start()
-
-            @pl.when(k == 2)
-            def _():
-                x_copy(1).wait_recv()
-                x_copy(5).start()
-
-            @pl.when(k == 4)
-            def _():
-                x_copy(2).wait_recv()
-                x_copy(6).start()
+                x_wait(0)
+                far_copy(0).start()
+                far_copy(1).start()
+
+            @pl.when(k == 3)
+            def _():
+                x_wait(1)
+                far_copy(2).start()
+                far_copy(3).start()
 
             @pl.when(k == 5)
             def _():
-                x_copy(3).wait_recv()
-                x_copy(7).start()
+                far_copy(2).wait_recv()
+                far_copy(3).wait_recv()
 
             @pl.when(k == 6)
             def _():
-                x_copy(6).wait_recv()
-                x_copy(7).wait_recv()
-
-            @pl.when(k == 7)
-            def _():
-                x_copy(4).wait_recv()
-                x_copy(5).wait_recv()
+                far_copy(0).wait_recv()
+                far_copy(1).wait_recv()
 
             project(k)
 
-        @pl.when((t >= up_end + PER) & ((t - up_end) % PER == 0))
-        def _():
-            k = (t - up_end) // PER - 1
-            back(k)
-
-            @pl.when(k == CHUNKS - 1)
-            def _():
-                grads, terms = collect(1)
-                z_send[...] = grads.astype(BF16)
-                t_send[...] = terms
-                for copy in last:
-                    copy.start()
-
-            @pl.when(k % 2 == 1)
-            def _():
-                weights(k // 2)
+        u = t - up_end
+
+        @pl.when((u >= PER) & (u % PER == 0))
+        def _():
+            back(u // PER - 1)
+
+        v = u - 2 * PER
+        j, m = v // (2 * PER), v % (2 * PER)
+
+        @pl.when((v > 0) & ((m == 1) | (m == 2) | (m == 5) | (m == 6)))
+        def _():
+            q = jnp.where(m < 3, m - 1, m - 3)
+
+            @pl.when(q == 0)
+            def _():
+                weights_in(j)
+
+            weights(j, q)
+
+        @pl.when(u == 6 * PER + PER - 1)
+        def _():
+            z_send[...] = collect(1).astype(BF16)
+            last.start()
+
+            @pl.when(root)
+            def _():
+                t_send[...] = collect_terms(1)
+                last_term.start()
+
+        @pl.when((u == 8 * PER - 1) & root)
+        def _():
+            terms = collect_terms(0)
+            last_term.wait_recv()
+            term_all[slot] = terms + t_recv[...]
+            for o in range(1, 8):
+                all_copy(o).start()
 
         return carry
 
     lax.fori_loop(0, NSUB + up_end + 1, tick, 0)
 
-    grads, terms = collect(0)
-    for copy in last:
-        copy.wait_recv()
+    weights_in(CHUNKS // 2 - 1)
+
+    def ending(q, carry):
+        weights(CHUNKS // 2 - 1, q)
+        return carry
+
+    lax.fori_loop(0, 4, ending, 0)
+    grads = collect(0)
+    last.wait_recv()
     out_x[...] = (grads + z_recv[...].astype(F32)).astype(BF16)
-    out_p[...] = terms + t_recv[...]
-
-    for copy in last:
-        copy.wait_send()
+    for i in range(4):
+        source = (0, 1, 6, 7)[i]
+
+        @pl.when(tensor != source)
+        def _():
+            part = term_all.at[i]
+            remote(part, part, all_s.at[0], all_r.at[i], partner).wait_recv()
+
+    out_p[...] = term_all[0] + term_all[1] + term_all[2] + term_all[3]
+    last.wait_send()
+
+    @pl.when(root)
+    def _():
+        last_term.wait_send()
+        for o in range(1, 8):
+            all_copy(o).wait_send()
+
+        def drain_terms(s, carry):
+            zi, step = chunk_place(s // PER)
+
+            @pl.when(jnp.logical_not((s % PER == 0) & (step == 0)))
+            def _():
+                term_copy(s).wait_send()
+
+            return carry
+
+        lax.fori_loop(0, NSUB, drain_terms, 0)
+
     for copy in raw:
         copy.wait_send()
     for z in range(2):
         for o in (1, 2, 3):
             y_copy(z, o).wait_send()
-    for i in range(8):
-        x_copy(i).wait_send()
+        for side in range(2):
+            for g in range(4):
+                x_copy(z, side, g).wait_send()
+    for i in range(4):
+        far_copy(i).wait_send()
     for k in (CHUNKS - 2, CHUNKS - 1):
         for d in range(2):
             pair_copy(d, k).wait_send()
@@ -610,9 +713,9 @@
             vm((2, 2, ROWS, message), F32),
             vm((2, total, message), F32),
             vm((2, total, message), BF16),
-            vm((4, total, message + 128), BF16),
-            vm((2, ROWS, width + 128), BF16),
-            vm((2, 16, CAP, width + 128), BF16),
+            vm((4, total, message), BF16),
+            vm((2, ROWS, width), BF16),
+            vm((2, 16, CAP, width), BF16),
             vm((2, 16 * CAP, tok), BF16),
             vm((tok, width), BF16),
             vm((tok, width), BF16),
@@ -621,13 +724,19 @@
             vm((4, width, 2 * QUARTER), F32),
             vm((4, QUARTER, width), F32),
             vm((width, 2 * ROWS), BF16),
+            vm((2 * ROWS, width), BF16),
+            vm((NSUB, CAP, 128), BF16),
+            vm((2, 16, CAP, 128), BF16),
+            vm((4, 2, tok), F32),
             dma((9,)),
             dma((4,)),
             dma((4,)),
             dma((2, 4)),
             dma((2, 4)),
-            dma((8,)),
-            dma((8,)),
+            dma((2, 2, 4)),
+            dma((2, 2, 4)),
+            dma((4,)),
+            dma((4,)),
             dma((2, CHUNKS)),
             dma((2, CHUNKS)),
             dma((2, NSUB)),
@@ -640,6 +749,10 @@
             dma((2, 16)),
             dma((2,)),
             dma((2,)),
+            dma((NSUB,)),
+            dma((2, 16)),
+            dma((8,)),
+            dma((4,)),
         ],
         compiler_params=pltpu.CompilerParams(
             collective_id=0, has_side_effects=True, vmem_limit_bytes=55 * 1024 * 1024

time: 140 us -> 128 us (0.914)
  Pallas kernels: 135 us -> 122 us
    pallas_call x1, Pallas kernels: 135 us -> 122 us  [layer(): pl.pallas_call(functools.partial(kernel, width), out_shape=(vm((tok, widt...]
where the time goes in v3:
time: 128 us
  Pallas kernels  122 us (95%)
  local copies, waits for them, and re-layouts  4.62 us (4%)
    pallas_call x1, Pallas kernels, layer(): pl.pallas_call(functools.partial(kernel, width), out_shape=(vm((tok, widt...  122 us
    unnamed x5, local copies, waits for them, and re-layouts  4.62 us

profile of v3, /device:TPU:1, one launch (start us, length us, event | category | flops | bytes accessed | tf_op | source)
XLA Modules:
  0.0 127.6 jit_solution(11058191999392822176)
XLA Ops:
  0.6 122.3 %shard_map.110 = (bf16[48,768]{1,0:T(8,128)(2,1)S(1)}, f32[2,48]{1,0:T(2,128)S(1)}, bf16[768,1024]{1,0:T(8,128)(2,1)S(1)}, bf16[768,1024]{1,0:T(8,128)(2,1)S(1)}, bf16[1024,768]{1,0:T(8,128)(2,1)S(1)}) custom-call(bf16[48,768]{1,0:T(8,128)(2,1)} %tok_ref.1, bf16[48,768]{1,0:T(8,128)(2,1)} %grad_ref.1, s32[2,48]{1,0:T(2,128)} %bitcast.4, ...), custom_call_target="tpu_custom_call" | custom-call | tf_op jit(solution)/shard_map/pallas_call | solution.py:692
  122.9 0.6 copy.17
  123.6 0.6 copy.18
  124.1 1.1 copy.19
  125.3 1.1 copy.20
  126.4 1.1 copy.21

commit v4 on v3

--- a/solution.py
+++ b/solution.py
@@ -13,9 +13,13 @@
 ROWS = EXPERTS * CAP
 SUB = 32
 PER = ROWS // SUB
+PARTS = ((0, CAP, 0), (CAP, 2 * CAP, CHUNKS), (3 * CAP, CAP, CHUNKS + 1))
 NSUB = CHUNKS * PER
 LAG = 2
 QUARTER = 256
+TERMS_1 = 23
+TERMS_0 = 29
+TURN = 31
 MESH = pl.DeviceIdType.MESH
 F32 = jnp.float32
 BF16 = jnp.bfloat16
@@ -124,20 +128,13 @@
             src_ref=src, dst_ref=dst, send_sem=send, recv_sem=recv, device_id=device, device_id_type=MESH
         )
 
-    w_copies = []
     for q in range(4):
         cols = pl.ds(q * QUARTER, QUARTER)
-        w_copies.append(
-            pltpu.make_async_copy(wg_ref.at[:, cols], w_in.at[q, :, pl.ds(0, QUARTER)], w_sem.at[2 * q])
-        )
-        w_copies.append(
+        for i, ref in ((0, wg_ref), (1, wu_ref)):
             pltpu.make_async_copy(
-                wu_ref.at[:, cols], w_in.at[q, :, pl.ds(QUARTER, QUARTER)], w_sem.at[2 * q + 1]
-            )
-        )
-    w_copies.append(pltpu.make_async_copy(wd_ref, w_out, w_sem.at[8]))
-    for copy in w_copies:
-        copy.start()
+                ref.at[:, cols], w_in.at[q, :, pl.ds(i * QUARTER, QUARTER)], w_sem.at[0]
+            ).start()
+    pltpu.make_async_copy(wd_ref, w_out, w_sem.at[1]).start()
 
     barrier = pltpu.get_barrier_semaphore()
     for o in range(1, 16):
@@ -164,15 +161,15 @@
         g = (None, 2, 3, 1)[o]
         return remote(
             y_send.at[z, pl.ds(to * CAP, CAP)],
-            rows.at[2 * z, group(g)],
-            y_s.at[z, o],
+            rows.at[3 * z, group(g)],
+            y_s.at[z],
             y_r.at[z, g],
             at(to, zh, x),
         )
 
     def y_wait(z, g):
-        part = rows.at[2 * z, group(g)]
-        remote(part, part, y_s.at[z, 0], y_r.at[z, g], other_z).wait_recv()
+        part = rows.at[3 * z, group(g)]
+        remote(part, part, y_s.at[z], y_r.at[z, g], other_z).wait_recv()
 
     def choose(z, toks, grads, ids, probs):
         count = ids.shape[1]
@@ -197,10 +194,12 @@
         y_send[z, :, width:lanes] = dot(one, grads).astype(BF16)
         y_send[z, :, lanes : lanes + 128] = jnp.broadcast_to(prob, (ROWS, 128)).astype(BF16)
 
+    def place_own(z):
+        rows[3 * z, 0:CAP, :] = y_send[z, pl.ds(pl.multiple_of(y * CAP, CAP), CAP), :]
+
     def deal(z):
         for o in (1, 3, 2):
             y_copy(z, o).start()
-        rows[2 * z, 0:CAP, :] = y_send[z, pl.ds(pl.multiple_of(y * CAP, CAP), CAP), :]
         for side in range(2):
             x_copy(z, side, 0).start()
 
@@ -208,42 +207,46 @@
     half = ROWS // 2
 
     def x_copy(z, side, g):
-        dst = ((1, 7), (3, 4))[z][side]
+        dst = ((1, 2), (4, 6))[z][g // 2]
         return remote(
-            rows.at[2 * z, group(g)],
-            rows.at[dst, group(g)],
-            x_s.at[z, side, g],
-            x_r.at[z, side, g],
+            rows.at[3 * z, group(g)],
+            rows.at[dst, group(2 * side + g % 2)],
+            x_s.at[z],
+            x_r.at[z, g // 2],
             (right, left)[side],
         )
 
-    def x_pass(z):
-        for g in (1, 2, 3):
+    def x_pass(z, gs):
+        for g in gs:
             y_wait(z, g)
             for side in range(2):
                 x_copy(z, side, g).start()
 
-    def x_wait(z):
-        for side in range(2):
-            for g in range(4):
-                x_copy(z, side, g).wait_recv()
+    def x_wait(z, h):
+        part = rows.at[0]
+        remote(part, part, x_s.at[z], x_r.at[z, h], other_z).wait_recv()
 
     def far_copy(i):
         src, dst, lo, to = (
-            (1, 6, 0, right),
-            (7, 6, half, left),
-            (3, 5, 0, right),
-            (4, 5, half, left),
+            (1, 7, 0, right),
+            (2, 7, half, left),
+            (4, 5, 0, right),
+            (6, 5, half, left),
         )[i]
         part = pl.ds(lo, half)
-        return remote(rows.at[src, part], rows.at[dst, part], far_s.at[i], far_r.at[i], to)
-
-    def pair_copy(d, k):
+        return remote(rows.at[src, part], rows.at[dst, part], far_s.at[0], far_r.at[i // 2], to)
+
+    def far_wait(h):
+        part = rows.at[0]
+        remote(part, part, far_s.at[0], far_r.at[h], other_z).wait_recv()
+
+    def pair_copy(d, k, lo=0, n=ROWS, i=None):
+        i = k if i is None else i
         return remote(
-            pair_send.at[k % 2, d],
-            pair_recv.at[d, pl.ds(k * ROWS, ROWS)],
-            pair_s.at[d, k],
-            pair_r.at[d, k],
+            pair_send.at[k, d, pl.ds(lo, n)],
+            pair_recv.at[d, pl.ds(k * ROWS + lo, n)],
+            pair_s.at[d],
+            pair_r.at[d, i],
             partner,
         )
 
@@ -252,51 +255,54 @@
 
     def line_copy(d, s):
         part = line.at[d, sub_rows(s)]
-        return remote(part, part, line_s.at[d, s], line_r.at[d, s], below if d == 0 else above)
+        return remote(part, part, line_s.at[d], line_r.at[d, s], below if d == 0 else above)
 
     def cast_copy(d, s):
         part = hid.at[2 * d + core, sub_rows(s)]
-        return remote(part, part, cast_s.at[d, s], cast_r.at[d, s], above if d == 0 else below)
+        return remote(part, part, cast_s.at[d], cast_r.at[d, s], above if d == 0 else below)
 
     def core_copy(d, s):
         part = hid.at[2 * d + core, sub_rows(s)]
-        return remote(part, part, core_s.at[d, s], core_r.at[d, s], partner)
-
-    def core_wait(d, s):
-        part = hid.at[2 * d + 1 - core, sub_rows(s)]
-        remote(part, part, core_s.at[d, s], core_r.at[d, s], partner).wait_recv()
-
-    def project(k):
-        @pl.when(k >= 2)
-        def _():
-            for d in range(2):
-                pair_copy(d, k - 2).wait_send()
-
+        return remote(part, part, core_s.at[d], core_r.at[d, s // (PER // 2)], partner)
+
+    def core_wait(d, h):
+        part = hid.at[2 * d + 1 - core, pl.ds(pl.multiple_of(h * ROWS // 2, ROWS // 2), ROWS // 2)]
+        remote(part, part, core_s.at[d], core_r.at[d, h], partner).wait_recv()
+
+    def project(k, lo=0, n=ROWS, i=None):
+        take = pl.ds(lo, n)
         for d in range(2):
             for mine in (False, True):
                 q = 2 * d + (core if mine else 1 - core)
-                up = dot(rows[k, :, 0:width], w_in[q])
+                up = dot(rows[k, take, 0:width], w_in[q])
                 back = dot_nt(
-                    rows[k, :, width:lanes],
+                    rows[k, take, width:lanes],
                     w_out[pl.ds(pl.multiple_of(q * QUARTER, QUARTER), QUARTER), :],
                 )
                 if mine:
-                    part = pl.ds(pl.multiple_of(k * ROWS, ROWS), ROWS)
+                    part = pl.ds(pl.multiple_of(k * ROWS + lo, CAP), n)
                     own[d, part, 0 : 2 * QUARTER] = up
                     own[d, part, 2 * QUARTER : 3 * QUARTER] = back
                 else:
-                    pair_send[k % 2, d, :, 0 : 2 * QUARTER] = up
-                    pair_send[k % 2, d, :, 2 * QUARTER : 3 * QUARTER] = back
-                    pair_copy(d, k).start()
+                    pair_send[k, d, take, 0 : 2 * QUARTER] = up
+                    pair_send[k, d, take, 2 * QUARTER : 3 * QUARTER] = back
+                    if i != 0:
+                        pair_copy(d, k, lo, n, i).start()
 
     def reduce(d, s):
         place = 3 - zl if d == 0 else zl
 
         @pl.when((s >= 0) & (s < NSUB))
         def _():
-            @pl.when(s % PER == 0)
+            @pl.when((s % PER == 0) & (s > 0))
             def _():
                 pair_copy(d, s // PER).wait_recv()
+
+            for lo, n, i in PARTS:
+
+                @pl.when(s == lo // SUB)
+                def _():
+                    pair_copy(d, 0, lo, n, i).wait_recv()
 
             part = sub_rows(s)
 
@@ -335,7 +341,7 @@
                 cast_copy(d, s).start()
                 core_copy(d, s).start()
                 term_send[s] = two_parts(term, SUB)
-                zi, step = chunk_place(s // PER)
+                zi, _, step = chunk_place(s // PER, s % PER)
                 self_too = (s % PER == 0) & (step == 0)
 
                 @pl.when(self_too)
@@ -347,13 +353,12 @@
                     term_copy(s).start()
 
     def term_copy(s):
-        zi, step = chunk_place(s // PER)
-        to_y = (y + offset(s % PER)) % 4
+        zi, to_y, step = chunk_place(s // PER, s % PER)
         return remote(
             term_send.at[s],
             term_recv.at[zi, here],
-            term_s.at[s],
-            term_r.at[zi, here],
+            term_s.at[0],
+            term_r.at[zi],
             at(to_y, zh, (x + step) % 4),
         )
 
@@ -375,69 +380,55 @@
 
             core_copy(d, s).start()
 
-    def chunk_place(k):
-        zi = jnp.where((k >= 2) & (k < 6), 1, 0)
-        step = jnp.where(
-            (k == 0) | (k == 2), 0, jnp.where((k == 1) | (k == 3), 3, jnp.where((k == 4) | (k == 7), 1, 2))
-        )
-        return zi, step
+    def chunk_place(k, g):
+        zi = jnp.where((k >= 3) & (k < 7), 1, 0)
+        late = (k == 2) | (k == 6)
+        near = late | (k == 1) | (k == 4)
+        far = (k == 5) | (k == 7)
+        step = jnp.where(near, jnp.where(g < 2, 3, 1), jnp.where(far, 2, 0))
+        source = jnp.where(near, g % 2 + jnp.where(late, 2, 0), g)
+        return zi, (y + offset(source)) % 4, step
 
     def ret_copy(k, g):
-        zi, step = chunk_place(k)
-        to_y = (y + (0, 1, 3, 2)[g]) % 4
+        zi, to_y, step = chunk_place(k, g)
         return remote(
-            ret_send.at[k % 2, group(g)],
+            ret_send.at[k, group(g)],
             ret_recv.at[zi, here],
-            ret_s.at[k, g],
-            ret_r.at[zi, here],
+            ret_s.at[0],
+            ret_r.at[zi],
             at(to_y, zh, (x + step) % 4),
         )
 
-    def ret_wait(zi, o):
-        source = (here + o) % 16
-        remote(
-            ret_send.at[0, pl.ds(0, CAP)],
-            ret_recv.at[zi, source],
-            ret_s.at[0, 0],
-            ret_r.at[zi, source],
-            plane(source),
-        ).wait_recv()
-
-    def ret_done(k):
-        zi, step = chunk_place(k)
-
-        @pl.when(step != 0)
-        def _():
-            ret_copy(k, 0).wait_send()
-
-        for o in (1, 2, 3):
-            ret_copy(k, o).wait_send()
-
-    def back(k):
+    def ret_wait(zi):
+        part = ret_recv.at[zi, pl.ds(0, 15)]
+        remote(part, part, ret_s.at[0], ret_r.at[zi], other_z).wait_recv()
+
+    def back(k, lo=0, n=ROWS):
         for d in range(2):
-            for i in range(PER):
-                core_wait(d, k * PER + i)
-
-        @pl.when(k >= 2)
-        def _():
-            ret_done(k - 2)
-
-        part = pl.ds(pl.multiple_of(k * ROWS, ROWS), ROWS)
+            for h in range(2):
+                if lo <= h * (ROWS // 2) < lo + n:
+                    core_wait(d, 2 * k + h)
+
+        take = pl.ds(lo, n)
+        part = pl.ds(pl.multiple_of(k * ROWS + lo, ROWS // 2), n)
         total = dot_nt(hid[0, part, QUARTER : 3 * QUARTER], w_in[0])
         for q in range(1, 4):
             total += dot_nt(hid[q, part, QUARTER : 3 * QUARTER], w_in[q])
-        ret_send[k % 2] = total.astype(BF16)
-        zi, step = chunk_place(k)
+        ret_send[k, take, :] = total.astype(BF16)
+        zi, _, step = chunk_place(k, 0)
         for g in (3, 1, 2):
-            ret_copy(k, g).start()
-
-        @pl.when(step != 0)
-        def _():
-            ret_copy(k, 0).start()
-
-        @pl.when(step == 0)
-        def _():
-            ret_recv[zi, here] = ret_send[k % 2, 0:CAP, :]
+            if lo <= g * CAP < lo + n:
+                ret_copy(k, g).start()
+
+        if lo == 0:
+
+            @pl.when(step != 0)
+            def _():
+                ret_copy(k, 0).start()
+
+            @pl.when(step == 0)
+            def _():
+                ret_recv[zi, here] = ret_send[k, 0:CAP, :]
 
     def weights_in(j):
         two = pl.ds(2 * j, 2)
@@ -469,14 +460,16 @@
             out_d[cols, :] = (acc_out[q] + down).astype(BF16)
 
     choose(0, tok_ref[...], grad_ref[...], ids_ref[...], prob_ref[...].astype(F32))
+    place_own(0)
+    pltpu.make_async_copy(w_in, w_in, w_sem.at[0]).wait()
+    pltpu.make_async_copy(w_out, w_out, w_sem.at[1]).wait()
+    project(0, *PARTS[0])
     pl.semaphore_wait(barrier, 23)
     deal(0)
+    for d in range(2):
+        pair_copy(d, 0, *PARTS[0]).start()
     for copy in raw:
         copy.start()
-    x_pass(0)
-    for copy in w_copies:
-        copy.wait()
-    project(0)
 
     def chosen(zi):
         p = p_all[zi]
@@ -489,16 +482,13 @@
             pick[1, part, :] = second[e : e + CAP, :]
 
     def collect(zi):
-        for o in range(1, 16):
-            ret_wait(zi, o)
+        ret_wait(zi)
         chosen(zi)
         return dot_tn(pick[0] + pick[1], ret_recv[zi].reshape(16 * CAP, width))
 
     def collect_terms(zi):
-        for o in range(1, 16):
-            source = (here + o) % 16
-            part = term_recv.at[zi, source]
-            remote(part, part, term_s.at[0], term_r.at[zi, source], plane(source)).wait_recv()
+        part = term_recv.at[zi, pl.ds(0, 15)]
+        remote(part, part, term_s.at[0], term_r.at[zi], other_z).wait_recv()
         chosen(zi)
         got = term_recv[zi].reshape(16 * CAP, 128)
         terms = [dot_tn(got, pick[i]) for i in range(2)]
@@ -511,8 +501,8 @@
         return remote(
             term_all.at[slot],
             term_all.at[slot],
-            all_s.at[o],
-            all_r.at[slot],
+            all_s.at[0],
+            all_r.at[0],
             (dp, (tensor + o) % 8),
         )
 
@@ -529,55 +519,73 @@
             place = 3 - zl if d == 0 else zl
             reduce(d, t - LAG * place)
 
-        @pl.when(t == 1)
-        def _():
+        @pl.when(t == 0)
+        def _():
+            x_pass(0, (1, 2))
+            project(0, *PARTS[1])
+
+        @pl.when(t == 2)
+        def _():
+            x_pass(0, (3,))
+            project(0, *PARTS[2])
             for copy in raw:
                 copy.wait_recv()
             choose(1, x_other[0], x_other[1], ids_other[...], prob_other[...].astype(F32))
+            place_own(1)
             deal(1)
 
-        @pl.when(t == PER + 1)
-        def _():
-            x_pass(1)
-
-        @pl.when(((t + 1) % PER == 0) & (t + 1 < NSUB))
+        @pl.when(t == 2 * PER)
+        def _():
+            x_pass(1, (1, 2, 3))
+
+        @pl.when(t == 4 * PER)
+        def _():
+            x_wait(1, 1)
+            far_copy(3).start()
+
+        @pl.when((t % PER == PER - 1) & (t + 1 < NSUB))
         def _():
             k = (t + 1) // PER
 
             @pl.when(k == 1)
             def _():
-                x_wait(0)
+                x_wait(0, 0)
                 far_copy(0).start()
+
+            @pl.when(k == 2)
+            def _():
+                x_wait(0, 1)
                 far_copy(1).start()
 
-            @pl.when(k == 3)
-            def _():
-                x_wait(1)
+            @pl.when(k == 4)
+            def _():
+                x_wait(1, 0)
                 far_copy(2).start()
-                far_copy(3).start()
 
             @pl.when(k == 5)
             def _():
-                far_copy(2).wait_recv()
-                far_copy(3).wait_recv()
-
-            @pl.when(k == 6)
-            def _():
-                far_copy(0).wait_recv()
-                far_copy(1).wait_recv()
+                far_wait(1)
+
+            @pl.when(k == 7)
+            def _():
+                far_wait(0)
 
             project(k)
 
         u = t - up_end
 
-        @pl.when((u >= PER) & (u % PER == 0))
+        @pl.when((u >= PER) & (u % PER == 0) & (u < 8 * PER))
         def _():
             back(u // PER - 1)
+
+        @pl.when(u == 8 * PER - 2)
+        def _():
+            back(CHUNKS - 1, 0, ROWS // 2)
 
         v = u - 2 * PER
         j, m = v // (2 * PER), v % (2 * PER)
 
-        @pl.when((v > 0) & ((m == 1) | (m == 2) | (m == 5) | (m == 6)))
+        @pl.when((v > 0) & (v < 5 * PER) & ((m == 1) | (m == 2) | (m == 5) | (m == 6)))
         def _():
             q = jnp.where(m < 3, m - 1, m - 3)
 
@@ -587,17 +595,16 @@
 
             weights(j, q)
 
-        @pl.when(u == 6 * PER + PER - 1)
-        def _():
-            z_send[...] = collect(1).astype(BF16)
-            last.start()
-
-            @pl.when(root)
-            def _():
-                t_send[...] = collect_terms(1)
-                last_term.start()
-
-        @pl.when((u == 8 * PER - 1) & root)
+        @pl.when(u == 8 * PER)
+        def _():
+            back(CHUNKS - 1, ROWS // 2, ROWS // 2)
+
+        @pl.when((u == TERMS_1) & root)
+        def _():
+            t_send[...] = collect_terms(1)
+            last_term.start()
+
+        @pl.when((u == TERMS_0) & root)
         def _():
             terms = collect_terms(0)
             last_term.wait_recv()
@@ -605,10 +612,17 @@
             for o in range(1, 8):
                 all_copy(o).start()
 
+        @pl.when(u == TURN)
+        def _():
+            z_send[...] = collect(1).astype(BF16)
+            last.start()
+
         return carry
 
     lax.fori_loop(0, NSUB + up_end + 1, tick, 0)
 
+    weights(CHUNKS // 2 - 2, 2)
+    weights(CHUNKS // 2 - 2, 3)
     weights_in(CHUNKS // 2 - 1)
 
     def ending(q, carry):
@@ -619,13 +633,16 @@
     grads = collect(0)
     last.wait_recv()
     out_x[...] = (grads + z_recv[...].astype(F32)).astype(BF16)
-    for i in range(4):
-        source = (0, 1, 6, 7)[i]
-
-        @pl.when(tensor != source)
-        def _():
-            part = term_all.at[i]
-            remote(part, part, all_s.at[0], all_r.at[i], partner).wait_recv()
+
+    @pl.when(root)
+    def _():
+        part = term_all.at[pl.ds(0, 3)]
+        remote(part, part, all_s.at[0], all_r.at[0], partner).wait_recv()
+
+    @pl.when(jnp.logical_not(root))
+    def _():
+        part = term_all.at[pl.ds(0, 4)]
+        remote(part, part, all_s.at[0], all_r.at[0], partner).wait_recv()
 
     out_p[...] = term_all[0] + term_all[1] + term_all[2] + term_all[3]
     last.wait_send()
@@ -633,51 +650,39 @@
     @pl.when(root)
     def _():
         last_term.wait_send()
-        for o in range(1, 8):
-            all_copy(o).wait_send()
-
-        def drain_terms(s, carry):
-            zi, step = chunk_place(s // PER)
-
-            @pl.when(jnp.logical_not((s % PER == 0) & (step == 0)))
-            def _():
-                term_copy(s).wait_send()
-
-            return carry
-
-        lax.fori_loop(0, NSUB, drain_terms, 0)
+        part = term_all.at[pl.ds(0, 7)]
+        remote(part, part, all_s.at[0], all_r.at[0], partner).wait_send()
+
+        part = term_recv.at[:, pl.ds(0, 15)]
+        remote(part, part, term_s.at[0], term_r.at[0], other_z).wait_send()
 
     for copy in raw:
         copy.wait_send()
     for z in range(2):
-        for o in (1, 2, 3):
-            y_copy(z, o).wait_send()
-        for side in range(2):
-            for g in range(4):
-                x_copy(z, side, g).wait_send()
-    for i in range(4):
-        far_copy(i).wait_send()
-    for k in (CHUNKS - 2, CHUNKS - 1):
-        for d in range(2):
-            pair_copy(d, k).wait_send()
-        ret_done(k)
-
-    def drain(s, carry):
-        for d in range(2):
-            place = 3 - zl if d == 0 else zl
-
-            @pl.when(place < 3)
-            def _():
-                line_copy(d, s).wait_send()
-
-            @pl.when(place > 0)
-            def _():
-                cast_copy(d, s).wait_send()
-
-            core_copy(d, s).wait_send()
-        return carry
-
-    lax.fori_loop(0, NSUB, drain, 0)
+        part = rows.at[0, pl.ds(0, 3 * CAP)]
+        remote(part, part, y_s.at[z], y_r.at[z, 0], other_z).wait_send()
+        part = rows.at[pl.ds(0, 2)]
+        remote(part, part, x_s.at[z], x_r.at[z, 0], other_z).wait_send()
+    part = rows.at[pl.ds(0, 2)]
+    remote(part, part, far_s.at[0], far_r.at[0], other_z).wait_send()
+    for d in range(2):
+        part = pair_recv.at[d]
+        remote(part, part, pair_s.at[d], pair_r.at[d, 0], partner).wait_send()
+    part = ret_recv.at[:, pl.ds(0, 15)]
+    remote(part, part, ret_s.at[0], ret_r.at[0], other_z).wait_send()
+    for d in range(2):
+        place = 3 - zl if d == 0 else zl
+        whole = hid.at[0]
+
+        @pl.when(place < 3)
+        def _():
+            remote(line.at[d], line.at[d], line_s.at[d], line_r.at[d, 0], partner).wait_send()
+
+        @pl.when(place > 0)
+        def _():
+            remote(whole, whole, cast_s.at[d], cast_r.at[d, 0], partner).wait_send()
+
+        remote(whole, whole, core_s.at[d], core_r.at[d, 0], partner).wait_send()
 
 
 def layer(tokens, out_grad, ids, probs, gate_weight, up_weight, down_weight):
@@ -710,11 +715,11 @@
             vm((4, width, 2 * QUARTER), BF16),
             vm((hid, width), BF16),
             vm((2, total, message), F32),
-            vm((2, 2, ROWS, message), F32),
+            vm((CHUNKS, 2, ROWS, message), F32),
             vm((2, total, message), F32),
             vm((2, total, message), BF16),
             vm((4, total, message), BF16),
-            vm((2, ROWS, width), BF16),
+            vm((CHUNKS, ROWS, width), BF16),
             vm((2, 16, CAP, width), BF16),
             vm((2, 16 * CAP, tok), BF16),
             vm((tok, width), BF16),
@@ -727,32 +732,32 @@
             vm((2 * ROWS, width), BF16),
             vm((NSUB, CAP, 128), BF16),
             vm((2, 16, CAP, 128), BF16),
-            vm((4, 2, tok), F32),
-            dma((9,)),
+            vm((8, 2, tok), F32),
+            dma((2,)),
             dma((4,)),
             dma((4,)),
+            dma((2,)),
             dma((2, 4)),
-            dma((2, 4)),
-            dma((2, 2, 4)),
-            dma((2, 2, 4)),
-            dma((4,)),
-            dma((4,)),
-            dma((2, CHUNKS)),
-            dma((2, CHUNKS)),
+            dma((2,)),
+            dma((2, 2)),
+            dma((1,)),
+            dma((2,)),
+            dma((2,)),
+            dma((2, CHUNKS + 2)),
+            dma((2,)),
             dma((2, NSUB)),
+            dma((2,)),
             dma((2, NSUB)),
-            dma((2, NSUB)),
-            dma((2, NSUB)),
-            dma((2, NSUB)),
-            dma((2, NSUB)),
-            dma((CHUNKS, 4)),
-            dma((2, 16)),
-            dma((2,)),
-            dma((2,)),
-            dma((NSUB,)),
-            dma((2, 16)),
-            dma((8,)),
-            dma((4,)),
+            dma((2,)),
+            dma((2, 2 * CHUNKS)),
+            dma((1,)),
+            dma((2,)),
+            dma((2,)),
+            dma((2,)),
+            dma((1,)),
+            dma((2,)),
+            dma((1,)),
+            dma((1,)),
         ],
         compiler_params=pltpu.CompilerParams(
             collective_id=0, has_side_effects=True, vmem_limit_bytes=55 * 1024 * 1024
@@ -760,9 +765,30 @@
     )(tokens, out_grad, ids, probs, gate_weight, up_weight, down_weight)
 
 
+def spill(*refs):
+    n = len(refs) // 2
+    sems = refs[-1]
+    copies = [pltpu.make_async_copy(refs[i], refs[n + i], sems.at[i]) for i in range(n)]
+    for copy in copies:
+        copy.start()
+    for copy in copies:
+        copy.wait()
+
+
+def put(arrays):
+    return pl.pallas_call(
+        spill,
+        out_shape=tuple(pltpu.HBM(a.shape, a.dtype) for a in arrays),
+        in_specs=[pl.BlockSpec(memory_space=pltpu.VMEM)] * len(arrays),
+        out_specs=(pl.BlockSpec(memory_space=pltpu.HBM),) * len(arrays),
+        scratch_shapes=[pltpu.SemaphoreType.DMA((len(arrays),))],
+        compiler_params=pltpu.CompilerParams(vmem_limit_bytes=16 * 1024 * 1024),
+    )(*arrays)
+
+
 def body(tokens, out_grad, expert_ids, gate_prob, gate_weight, up_weight, down_weight):
-    input_grad, terms, gate_grad, up_grad, down_grad = layer(
-        tokens, out_grad, expert_ids.T, gate_prob.T, gate_weight, up_weight, down_weight
+    input_grad, terms, gate_grad, up_grad, down_grad = put(
+        layer(tokens, out_grad, expert_ids.T, gate_prob.T, gate_weight, up_weight, down_weight)
     )
     return (input_grad, terms.T, gate_grad, up_grad, down_grad)
 

time: 128 us -> 116 us (0.906)
  Pallas kernels: 122 us -> 114 us
  local copies, waits for them, and re-layouts: 4.62 us -> 0 us
    pallas_call x1, Pallas kernels: 122 us -> 112 us  [layer(): pl.pallas_call(functools.partial(kernel, width), out_shape=(vm((tok, widt...]
    unnamed x5 -> x0, local copies, waits for them, and re-layouts: 4.62 us -> none
    pallas_call x0 -> x1, Pallas kernels: none -> 2.25 us  [put(): pl.pallas_call(spill, out_shape=tuple((pltpu.HBM(a.shape, a.dtype) for a...]
where the time goes in v4:
time: 116 us; the launch traced here: 115 us
  Pallas kernels  114 us (98%)
    pallas_call x1, Pallas kernels, layer(): pl.pallas_call(functools.partial(kernel, width), out_shape=(vm((tok, widt...  112 us

profile of v4, /device:TPU:1, one launch (start us, length us, event | category | flops | bytes accessed | tf_op | source)
XLA Modules:
  0.0 115.0 jit_solution(4478553625722023377)
XLA Ops:
  0.6 112.1 %shard_map.110 = (bf16[48,768]{1,0:T(8,128)(2,1)S(1)}, f32[2,48]{1,0:T(2,128)S(1)}, bf16[768,1024]{1,0:T(8,128)(2,1)S(1)}, bf16[768,1024]{1,0:T(8,128)(2,1)S(1)}, bf16[1024,768]{1,0:T(8,128)(2,1)S(1)}) custom-call(bf16[48,768]{1,0:T(8,128)(2,1)} %tok_ref.1, bf16[48,768]{1,0:T(8,128)(2,1)} %grad_ref.1, s32[2,48]{1,0:T(2,128)} %bitcast.3, ...), custom_call_target="tpu_custom_call" | custom-call | tf_op jit(solution)/shard_map/pallas_call | solution.py:697
  112.8 2.3 %shard_map.111 = (bf16[48,768]{1,0:T(8,128)(2,1)}, f32[2,48]{1,0:T(2,128)}, bf16[768,1024]{1,0:T(8,128)(2,1)}, bf16[768,1024]{1,0:T(8,128)(2,1)}, bf16[1024,768]{1,0:T(8,128)(2,1)}) custom-call(bf16[48,768]{1,0:T(8,128)(2,1)S(1)} %get-tuple-element.15.refs_0_, f32[2,48]{1,0:T(2,128)S(1)} %get-tuple-element.16.refs_1_, ...), custom_call_target="tpu_custom_call" | custom-call | tf_op jit(solution)/shard_map/pallas_call | solution.py:779

commit v5 on v4

--- a/solution.py
+++ b/solution.py
@@ -17,9 +17,8 @@
 NSUB = CHUNKS * PER
 LAG = 2
 QUARTER = 256
-TERMS_1 = 23
-TERMS_0 = 29
-TURN = 31
+TERMS_1 = 21
+TURN = 29
 MESH = pl.DeviceIdType.MESH
 F32 = jnp.float32
 BF16 = jnp.bfloat16
@@ -128,6 +127,13 @@
             src_ref=src, dst_ref=dst, send_sem=send, recv_sem=recv, device_id=device, device_id_type=MESH
         )
 
+    barrier = pltpu.get_barrier_semaphore()
+    pl.semaphore_signal(barrier, inc=1, device_id=other_z, device_id_type=MESH)
+    for o in range(1, 16):
+        pl.semaphore_signal(barrier, inc=1, device_id=plane((here + o) % 16), device_id_type=MESH)
+    for o in range(1, 8):
+        pl.semaphore_signal(barrier, inc=1, device_id=(dp, (tensor + o) % 8), device_id_type=MESH)
+
     for q in range(4):
         cols = pl.ds(q * QUARTER, QUARTER)
         for i, ref in ((0, wg_ref), (1, wu_ref)):
@@ -136,13 +142,6 @@
             ).start()
     pltpu.make_async_copy(wd_ref, w_out, w_sem.at[1]).start()
 
-    barrier = pltpu.get_barrier_semaphore()
-    for o in range(1, 16):
-        pl.semaphore_signal(barrier, inc=1, device_id=plane((here + o) % 16), device_id_type=MESH)
-    pl.semaphore_signal(barrier, inc=1, device_id=other_z, device_id_type=MESH)
-    for o in range(1, 8):
-        pl.semaphore_signal(barrier, inc=1, device_id=(dp, (tensor + o) % 8), device_id_type=MESH)
-
     raw = [
         remote(ids_ref, ids_other, z_s.at[0], z_r.at[0], other_z),
         remote(prob_ref, prob_other, z_s.at[1], z_r.at[1], other_z),
@@ -161,14 +160,14 @@
         g = (None, 2, 3, 1)[o]
         return remote(
             y_send.at[z, pl.ds(to * CAP, CAP)],
-            rows.at[3 * z, group(g)],
+            rows.at[2 * z, group(g)],
             y_s.at[z],
             y_r.at[z, g],
             at(to, zh, x),
         )
 
     def y_wait(z, g):
-        part = rows.at[3 * z, group(g)]
+        part = rows.at[2 * z, group(g)]
         remote(part, part, y_s.at[z], y_r.at[z, g], other_z).wait_recv()
 
     def choose(z, toks, grads, ids, probs):
@@ -195,7 +194,7 @@
         y_send[z, :, lanes : lanes + 128] = jnp.broadcast_to(prob, (ROWS, 128)).astype(BF16)
 
     def place_own(z):
-        rows[3 * z, 0:CAP, :] = y_send[z, pl.ds(pl.multiple_of(y * CAP, CAP), CAP), :]
+        rows[2 * z, 0:CAP, :] = y_send[z, pl.ds(pl.multiple_of(y * CAP, CAP), CAP), :]
 
     def deal(z):
         for o in (1, 3, 2):
@@ -207,10 +206,10 @@
     half = ROWS // 2
 
     def x_copy(z, side, g):
-        dst = ((1, 2), (4, 6))[z][g // 2]
+        dst = ((1, 7), (3, 5))[z][g // 2]
         return remote(
-            rows.at[3 * z, group(g)],
-            rows.at[dst, group(2 * side + g % 2)],
+            rows.at[2 * z, group(g)],
+            rows.at[dst, group(2 * side + g if g < 2 else 2 * (3 - g) + side)],
             x_s.at[z],
             x_r.at[z, g // 2],
             (right, left)[side],
@@ -227,14 +226,20 @@
         remote(part, part, x_s.at[z], x_r.at[z, h], other_z).wait_recv()
 
     def far_copy(i):
-        src, dst, lo, to = (
-            (1, 7, 0, right),
-            (2, 7, half, left),
-            (4, 5, 0, right),
-            (6, 5, half, left),
+        moves = (
+            ((1, 0, 6, 0, half),),
+            ((7, 3 * CAP, 6, 2 * CAP, CAP), (7, CAP, 6, 3 * CAP, CAP)),
+            ((3, 0, 4, 0, half),),
+            ((5, 3 * CAP, 4, 2 * CAP, CAP), (5, CAP, 4, 3 * CAP, CAP)),
         )[i]
-        part = pl.ds(lo, half)
-        return remote(rows.at[src, part], rows.at[dst, part], far_s.at[0], far_r.at[i // 2], to)
+        for src, at_src, dst, at_dst, n in moves:
+            remote(
+                rows.at[src, pl.ds(at_src, n)],
+                rows.at[dst, pl.ds(at_dst, n)],
+                far_s.at[0],
+                far_r.at[i // 2],
+                (right, left)[i % 2],
+            ).start()
 
     def far_wait(h):
         part = rows.at[0]
@@ -381,12 +386,13 @@
             core_copy(d, s).start()
 
     def chunk_place(k, g):
-        zi = jnp.where((k >= 3) & (k < 7), 1, 0)
-        late = (k == 2) | (k == 6)
-        near = late | (k == 1) | (k == 4)
-        far = (k == 5) | (k == 7)
-        step = jnp.where(near, jnp.where(g < 2, 3, 1), jnp.where(far, 2, 0))
-        source = jnp.where(near, g % 2 + jnp.where(late, 2, 0), g)
+        zi = jnp.where((k >= 2) & (k < 6), 1, 0)
+        late = (k == 5) | (k == 7)
+        near = late | (k == 1) | (k == 3)
+        far = (k == 4) | (k == 6)
+        side = jnp.where(late, g % 2, g // 2)
+        step = jnp.where(near, jnp.where(side == 0, 3, 1), jnp.where(far, 2, 0))
+        source = jnp.where(near, jnp.where(late, 3 - g // 2, g % 2), g)
         return zi, (y + offset(source)) % 4, step
 
     def ret_copy(k, g):
@@ -416,7 +422,7 @@
             total += dot_nt(hid[q, part, QUARTER : 3 * QUARTER], w_in[q])
         ret_send[k, take, :] = total.astype(BF16)
         zi, _, step = chunk_place(k, 0)
-        for g in (3, 1, 2):
+        for g in (2, 3, 1):
             if lo <= g * CAP < lo + n:
                 ret_copy(k, g).start()
 
@@ -528,50 +534,53 @@
         def _():
             x_pass(0, (3,))
             project(0, *PARTS[2])
+
+        @pl.when(t == PER + 1)
+        def _():
+            x_wait(0, 1)
+            far_copy(1)
+
+        @pl.when(t == 3 * PER)
+        def _():
+            x_wait(1, 1)
+            far_copy(3)
+
+        @pl.when((t % PER == PER - 1) & (t + 1 < NSUB))
+        def _():
+            k = (t + 1) // PER
+
+            @pl.when(k == 1)
+            def _():
+                x_wait(0, 0)
+                far_copy(0)
+
+            @pl.when(k == 2)
+            def _():
+                x_pass(1, (1, 2, 3))
+
+            @pl.when(k == 3)
+            def _():
+                x_wait(1, 0)
+                far_copy(2)
+
+            @pl.when(k == 4)
+            def _():
+                far_wait(1)
+
+            @pl.when(k == 6)
+            def _():
+                far_wait(0)
+
+            project(k)
+
+        @pl.when(t == PER - 1)
+        def _():
             for copy in raw:
                 copy.wait_recv()
             choose(1, x_other[0], x_other[1], ids_other[...], prob_other[...].astype(F32))
             place_own(1)
             deal(1)
 
-        @pl.when(t == 2 * PER)
-        def _():
-            x_pass(1, (1, 2, 3))
-
-        @pl.when(t == 4 * PER)
-        def _():
-            x_wait(1, 1)
-            far_copy(3).start()
-
-        @pl.when((t % PER == PER - 1) & (t + 1 < NSUB))
-        def _():
-            k = (t + 1) // PER
-
-            @pl.when(k == 1)
-            def _():
-                x_wait(0, 0)
-                far_copy(0).start()
-
-            @pl.when(k == 2)
-            def _():
-                x_wait(0, 1)
-                far_copy(1).start()
-
-            @pl.when(k == 4)
-            def _():
-                x_wait(1, 0)
-                far_copy(2).start()
-
-            @pl.when(k == 5)
-            def _():
-                far_wait(1)
-
-            @pl.when(k == 7)
-            def _():
-                far_wait(0)
-
-            project(k)
-
         u = t - up_end
 
         @pl.when((u >= PER) & (u % PER == 0) & (u < 8 * PER))
@@ -599,27 +608,27 @@
         def _():
             back(CHUNKS - 1, ROWS // 2, ROWS // 2)
 
+        @pl.when(u == TURN)
+        def _():
+            z_send[...] = collect(1).astype(BF16)
+            last.start()
+
         @pl.when((u == TERMS_1) & root)
         def _():
             t_send[...] = collect_terms(1)
             last_term.start()
 
-        @pl.when((u == TERMS_0) & root)
-        def _():
-            terms = collect_terms(0)
-            last_term.wait_recv()
-            term_all[slot] = terms + t_recv[...]
-            for o in range(1, 8):
-                all_copy(o).start()
-
-        @pl.when(u == TURN)
-        def _():
-            z_send[...] = collect(1).astype(BF16)
-            last.start()
-
         return carry
 
     lax.fori_loop(0, NSUB + up_end + 1, tick, 0)
+
+    @pl.when(root)
+    def _():
+        terms = collect_terms(0)
+        last_term.wait_recv()
+        term_all[slot] = terms + t_recv[...]
+        for o in range(1, 8):
+            all_copy(o).start()
 
     weights(CHUNKS // 2 - 2, 2)
     weights(CHUNKS // 2 - 2, 3)

time: 116 us -> 115 us (level); the launches traced: 115 us -> 115 us
  no operation moved by 1% of the time
where the time goes in v5:
time: 115 us
  Pallas kernels  115 us (100%)
    pallas_call x1, Pallas kernels, layer(): pl.pallas_call(functools.partial(kernel, width), out_shape=(vm((tok, widt...  112 us

profile of v5, /device:TPU:1, one launch (start us, length us, event | category | flops | bytes accessed | tf_op | source)
XLA Modules:
  0.0 115.3 jit_solution(2630145786609419077)
XLA Ops:
  0.6 112.4 %shard_map.110 = (bf16[48,768]{1,0:T(8,128)(2,1)S(1)}, f32[2,48]{1,0:T(2,128)S(1)}, bf16[768,1024]{1,0:T(8,128)(2,1)S(1)}, bf16[768,1024]{1,0:T(8,128)(2,1)S(1)}, bf16[1024,768]{1,0:T(8,128)(2,1)S(1)}) custom-call(bf16[48,768]{1,0:T(8,128)(2,1)} %tok_ref.1, bf16[48,768]{1,0:T(8,128)(2,1)} %grad_ref.1, s32[2,48]{1,0:T(2,128)} %bitcast.3, ...), custom_call_target="tpu_custom_call" | custom-call | tf_op jit(solution)/shard_map/pallas_call | solution.py:706
  113.1 2.3 %shard_map.111 = (bf16[48,768]{1,0:T(8,128)(2,1)}, f32[2,48]{1,0:T(2,128)}, bf16[768,1024]{1,0:T(8,128)(2,1)}, bf16[768,1024]{1,0:T(8,128)(2,1)}, bf16[1024,768]{1,0:T(8,128)(2,1)}) custom-call(bf16[48,768]{1,0:T(8,128)(2,1)S(1)} %get-tuple-element.15.refs_0_, f32[2,48]{1,0:T(2,128)S(1)} %get-tuple-element.16.refs_1_, ...), custom_call_target="tpu_custom_call" | custom-call | tf_op jit(solution)/shard_map/pallas_call | solution.py:788

commit v6 on v5

--- a/solution.py
+++ b/solution.py
@@ -14,8 +14,10 @@
 SUB = 32
 PER = ROWS // SUB
 PARTS = ((0, CAP, 0), (CAP, 2 * CAP, CHUNKS), (3 * CAP, CAP, CHUNKS + 1))
+LATER = ((0, 3 * CAP, 2), (3 * CAP, CAP, CHUNKS + 2))
 NSUB = CHUNKS * PER
 LAG = 2
+CAST = 2
 QUARTER = 256
 TERMS_1 = 21
 TURN = 29
@@ -197,7 +199,7 @@
         rows[2 * z, 0:CAP, :] = y_send[z, pl.ds(pl.multiple_of(y * CAP, CAP), CAP), :]
 
     def deal(z):
-        for o in (1, 3, 2):
+        for o in (1, 3, 2) if z == 0 else (1, 3):
             y_copy(z, o).start()
         for side in range(2):
             x_copy(z, side, 0).start()
@@ -299,9 +301,15 @@
 
         @pl.when((s >= 0) & (s < NSUB))
         def _():
-            @pl.when((s % PER == 0) & (s > 0))
+            @pl.when((s % PER == 0) & (s > 0) & (s != 2 * PER))
             def _():
                 pair_copy(d, s // PER).wait_recv()
+
+            for lo, n, i in LATER:
+
+                @pl.when(s == 2 * PER + lo // SUB)
+                def _():
+                    pair_copy(d, 2, lo, n, i).wait_recv()
 
             for lo, n, i in PARTS:
 
@@ -515,12 +523,12 @@
     last = remote(z_send, z_recv, last_s.at[0], last_r.at[0], other_z)
     last_term = remote(t_send, t_recv, last_s.at[1], last_r.at[1], other_z)
 
-    up_end = 6 * LAG
+    up_end = 3 * LAG + 3 * CAST
 
     def tick(t, carry):
         for d in range(2):
             place = 3 - zl if d == 0 else zl
-            spread(d, t - 3 * LAG - LAG * (3 - place))
+            spread(d, t - 3 * LAG - CAST * (3 - place))
         for d in range(2):
             place = 3 - zl if d == 0 else zl
             reduce(d, t - LAG * place)
@@ -537,6 +545,7 @@
 
         @pl.when(t == PER + 1)
         def _():
+            y_copy(1, 2).start()
             x_wait(0, 1)
             far_copy(1)
 
@@ -545,7 +554,17 @@
             x_wait(1, 1)
             far_copy(3)
 
-        @pl.when((t % PER == PER - 1) & (t + 1 < NSUB))
+        @pl.when(t == 2 * PER - 1)
+        def _():
+            x_pass(1, (1, 2))
+            project(2, *LATER[0])
+
+        @pl.when(t == 2 * PER + 1)
+        def _():
+            x_pass(1, (3,))
+            project(2, *LATER[1])
+
+        @pl.when((t % PER == PER - 1) & (t + 1 < NSUB) & (t != 2 * PER - 1))
         def _():
             k = (t + 1) // PER
 
@@ -553,10 +572,6 @@
             def _():
                 x_wait(0, 0)
                 far_copy(0)
-
-            @pl.when(k == 2)
-            def _():
-                x_pass(1, (1, 2, 3))
 
             @pl.when(k == 3)
             def _():
@@ -752,7 +767,7 @@
             dma((1,)),
             dma((2,)),
             dma((2,)),
-            dma((2, CHUNKS + 2)),
+            dma((2, CHUNKS + 3)),
             dma((2,)),
             dma((2, NSUB)),
             dma((2,)),

time: 115 us -> 114 us (level)
  Pallas kernels: 115 us -> 113 us
    pallas_call x1, Pallas kernels: 112 us -> 111 us  [layer(): pl.pallas_call(functools.partial(kernel, width), out_shape=(vm((tok, widt...]
where the time goes in v6:
time: 114 us; the launch traced here: 113 us
  Pallas kernels  113 us (99%)
    pallas_call x1, Pallas kernels, layer(): pl.pallas_call(functools.partial(kernel, width), out_shape=(vm((tok, widt...  111 us

profile of v6, /device:TPU:1, one launch (start us, length us, event | category | flops | bytes accessed | tf_op | source)
XLA Modules:
  0.0 113.5 jit_solution(18182703586673077482)
XLA Ops:
  0.6 110.6 %shard_map.110 = (bf16[48,768]{1,0:T(8,128)(2,1)S(1)}, f32[2,48]{1,0:T(2,128)S(1)}, bf16[768,1024]{1,0:T(8,128)(2,1)S(1)}, bf16[768,1024]{1,0:T(8,128)(2,1)S(1)}, bf16[1024,768]{1,0:T(8,128)(2,1)S(1)}) custom-call(bf16[48,768]{1,0:T(8,128)(2,1)} %tok_ref.1, bf16[48,768]{1,0:T(8,128)(2,1)} %grad_ref.1, s32[2,48]{1,0:T(2,128)} %bitcast.3, ...), custom_call_target="tpu_custom_call" | custom-call | tf_op jit(solution)/shard_map/pallas_call | solution.py:721
  111.2 2.3 %shard_map.111 = (bf16[48,768]{1,0:T(8,128)(2,1)}, f32[2,48]{1,0:T(2,128)}, bf16[768,1024]{1,0:T(8,128)(2,1)}, bf16[768,1024]{1,0:T(8,128)(2,1)}, bf16[1024,768]{1,0:T(8,128)(2,1)}) custom-call(bf16[48,768]{1,0:T(8,128)(2,1)S(1)} %get-tuple-element.15.refs_0_, f32[2,48]{1,0:T(2,128)S(1)} %get-tuple-element.16.refs_1_, ...), custom_call_target="tpu_custom_call" | custom-call | tf_op jit(solution)/shard_map/pallas_call | solution.py:803

commit v7 on v6

--- a/solution.py
+++ b/solution.py
@@ -546,6 +546,9 @@
         @pl.when(t == PER + 1)
         def _():
             y_copy(1, 2).start()
+
+        @pl.when(t == 2 * PER + 2)
+        def _():
             x_wait(0, 1)
             far_copy(1)
 

time: 114 us -> 114 us (level)
  no operation moved by 1% of the time
where the time goes in v7:
time: 114 us; the launch traced here: 113 us
  Pallas kernels  113 us (99%)
    pallas_call x1, Pallas kernels, layer(): pl.pallas_call(functools.partial(kernel, width), out_shape=(vm((tok, widt...  110 us

profile of v7, /device:TPU:1, one launch (start us, length us, event | category | flops | bytes accessed | tf_op | source)
XLA Modules:
  0.0 113.4 jit_solution(15101833033347780855)
XLA Ops:
  0.6 110.5 %shard_map.110 = (bf16[48,768]{1,0:T(8,128)(2,1)S(1)}, f32[2,48]{1,0:T(2,128)S(1)}, bf16[768,1024]{1,0:T(8,128)(2,1)S(1)}, bf16[768,1024]{1,0:T(8,128)(2,1)S(1)}, bf16[1024,768]{1,0:T(8,128)(2,1)S(1)}) custom-call(bf16[48,768]{1,0:T(8,128)(2,1)} %tok_ref.1, bf16[48,768]{1,0:T(8,128)(2,1)} %grad_ref.1, s32[2,48]{1,0:T(2,128)} %bitcast.3, ...), custom_call_target="tpu_custom_call" | custom-call | tf_op jit(solution)/shard_map/pallas_call | solution.py:724
  111.1 2.3 %shard_map.111 = (bf16[48,768]{1,0:T(8,128)(2,1)}, f32[2,48]{1,0:T(2,128)}, bf16[768,1024]{1,0:T(8,128)(2,1)}, bf16[768,1024]{1,0:T(8,128)(2,1)}, bf16[1024,768]{1,0:T(8,128)(2,1)}) custom-call(bf16[48,768]{1,0:T(8,128)(2,1)S(1)} %get-tuple-element.15.refs_0_, f32[2,48]{1,0:T(2,128)S(1)} %get-tuple-element.16.refs_1_, ...), custom_call_target="tpu_custom_call" | custom-call | tf_op jit(solution)/shard_map/pallas_call | solution.py:806
